TPU v7x, 8 devices: a whole 2x2x1 slice. The times are simulated.
8 devices in a mesh: dp: 1 (over z), tp: 2 (over y), cp: 4 (over x, core).
Axes of the slice: x: 2, y: 2, z: 1, core: 2. Of those that a mesh axis runs over, the one named last changes fastest.
Arguments:
- hidden: bfloat16 [2, 3072, 5376], P('dp', 'cp')
- cotangent: bfloat16 [2, 3072, 5376], P('dp', 'cp')
- positions: int32 [3072], P(('dp', 'cp'))
- w_q: bfloat16 [5376, 4096], P(None, 'tp')
- w_k: bfloat16 [5376, 2048], P(None, 'tp')
- w_v: bfloat16 [5376, 2048], P(None, 'tp')
- w_o: bfloat16 [4096, 5376], P('tp')
- w_pre: float32 [5376], replicated
- w_post: float32 [5376], replicated
- q_norm: float32 [128], replicated
- k_norm: float32 [128], replicated
Outputs:
- output 1: bfloat16 [2, 3072, 5376], P('dp', 'cp')
- output 2: bfloat16 [2, 3072, 5376], P('dp', 'cp')
- output 3: float32 [5376, 4096], P('dp', 'tp')
- output 4: float32 [5376, 2048], P('dp', 'tp')
- output 5: float32 [5376, 2048], P('dp', 'tp')
- output 6: float32 [4096, 5376], P(('dp', 'tp'))
- output 7: float32 [5376], P('dp')
- output 8: float32 [5376], P('dp')
- output 9: float32 [128], P('dp')
- output 10: float32 [128], P('dp')
All inputs are finite; a program needn't handle non-finite values.
Results may differ from a plain program's by a relative error of at most 0.02.
Values are sent between devices in bfloat16 or wider.
A program may use at most 1 GiB of HBM per device.

v0:
```python
import jax
import jax.numpy as jnp
from jax import lax
from jax.sharding import PartitionSpec as P

EPS = 1e-6
ROPE_BASE = 1000000.0
ROPE_SCALE = 8.0
NEG_BIG = -1e30


def rms_unit(values):
    inv_rms = lax.rsqrt(jnp.mean(values * values, axis=-1, keepdims=True) + EPS)
    return values * inv_rms, inv_rms


def rms_unit_back(d_unit, unit_vals, inv_rms):
    return inv_rms * (d_unit - unit_vals * jnp.mean(d_unit * unit_vals, axis=-1, keepdims=True))


def rope_tables(pos_loc, head_dim):
    half_dim = head_dim // 2
    inv_freq = 1.0 / (ROPE_SCALE * ROPE_BASE ** (jnp.arange(half_dim, dtype=jnp.float32) * (2.0 / head_dim)))
    angles = pos_loc.astype(jnp.float32)[:, None] * inv_freq[None, :]
    return jnp.cos(angles)[None, :, None, :], jnp.sin(angles)[None, :, None, :]


def rope_apply(values, cos_t, sin_t):
    half_dim = values.shape[-1] // 2
    lower_half = values[..., :half_dim]
    upper_half = values[..., half_dim:]
    return jnp.concatenate([lower_half * cos_t - upper_half * sin_t, upper_half * cos_t + lower_half * sin_t], axis=-1)


def rope_back(grads_in, cos_t, sin_t):
    half_dim = grads_in.shape[-1] // 2
    lower_half = grads_in[..., :half_dim]
    upper_half = grads_in[..., half_dim:]
    return jnp.concatenate([lower_half * cos_t + upper_half * sin_t, upper_half * cos_t - lower_half * sin_t], axis=-1)


def head_norm(raw_heads, norm_gain, cos_t, sin_t):
    unit_vals, inv_rms = rms_unit(raw_heads.astype(jnp.float32))
    final_heads = rope_apply(unit_vals * (1.0 + norm_gain), cos_t, sin_t).astype(jnp.bfloat16)
    return final_heads, unit_vals, inv_rms


def head_norm_back(d_final, norm_gain, unit_vals, inv_rms, cos_t, sin_t):
    d_scaled = rope_back(d_final, cos_t, sin_t)
    d_gain = jnp.sum(d_scaled * unit_vals, axis=(0, 1, 2))
    return rms_unit_back(d_scaled * (1.0 + norm_gain), unit_vals, inv_rms), d_gain


def attend_block(run_stats, q_fin, k_blk, v_blk, q_pos, k_pos, score_scale):
    run_max, run_sum, run_acc = run_stats
    scores = jnp.einsum('bqkgd,bskd->bkgqs', q_fin, k_blk, preferred_element_type=jnp.float32) * score_scale
    allowed = k_pos[None, :] <= q_pos[:, None]
    new_max = jnp.maximum(run_max, jnp.max(jnp.where(allowed, scores, NEG_BIG), axis=-1))
    attn_prob = jnp.where(allowed, jnp.exp(scores - new_max[..., None]), 0.0)
    factor = jnp.exp(run_max - new_max)
    new_sum = run_sum * factor + jnp.sum(attn_prob, axis=-1)
    new_acc = run_acc * factor[..., None] + jnp.einsum('bkgqs,bskd->bkgqd', attn_prob.astype(jnp.bfloat16), v_blk, preferred_element_type=jnp.float32)
    return new_max, new_sum, new_acc


def grad_block(q_fin, d_out, log_norm, row_delta, q_pos, k_blk, v_blk, k_pos, score_scale):
    scores = jnp.einsum('bqkgd,bskd->bkgqs', q_fin, k_blk, preferred_element_type=jnp.float32) * score_scale
    allowed = k_pos[None, :] <= q_pos[:, None]
    attn_prob = jnp.where(allowed, jnp.exp(scores - log_norm[..., None]), 0.0)
    grad_v = jnp.einsum('bkgqs,bkgqd->bskd', attn_prob.astype(jnp.bfloat16), d_out, preferred_element_type=jnp.float32)
    d_prob = jnp.einsum('bkgqd,bskd->bkgqs', d_out, v_blk, preferred_element_type=jnp.float32)
    d_score = (attn_prob * (d_prob - row_delta[..., None]) * score_scale).astype(jnp.bfloat16)
    grad_q = jnp.einsum('bkgqs,bskd->bqkgd', d_score, k_blk, preferred_element_type=jnp.float32)
    grad_k = jnp.einsum('bkgqs,bqkgd->bskd', d_score, q_fin, preferred_element_type=jnp.float32)
    return grad_q, grad_k, grad_v


def solution(mesh):
    n_cp = mesh.shape['cp']
    next_hop = [(dev_idx, (dev_idx + 1) % n_cp) for dev_idx in range(n_cp)]

    def per_device(hidden, cotangent, pos_loc, w_q, w_k, w_v, w_o, w_pre, w_post, q_norm, k_norm):
        head_dim = q_norm.shape[0]
        n_batch, seq_loc, model_dim = hidden.shape
        q_heads = w_q.shape[1] // head_dim
        kv_heads = w_k.shape[1] // head_dim
        groups = q_heads // kv_heads
        score_scale = head_dim ** -0.5
        cos_t, sin_t = rope_tables(pos_loc, head_dim)

        x_f32 = hidden.astype(jnp.float32)
        x_unit, x_inv = rms_unit(x_f32)
        normed = (x_unit * (1.0 + w_pre)).astype(jnp.bfloat16)
        q_raw = jnp.einsum('bsd,dh->bsh', normed, w_q, preferred_element_type=jnp.float32).astype(jnp.bfloat16).reshape(n_batch, seq_loc, q_heads, head_dim)
        k_raw = jnp.einsum('bsd,dh->bsh', normed, w_k, preferred_element_type=jnp.float32).astype(jnp.bfloat16).reshape(n_batch, seq_loc, kv_heads, head_dim)
        v_loc = jnp.einsum('bsd,dh->bsh', normed, w_v, preferred_element_type=jnp.float32).astype(jnp.bfloat16).reshape(n_batch, seq_loc, kv_heads, head_dim)
        q_fin, q_unit, q_inv = head_norm(q_raw, q_norm, cos_t, sin_t)
        k_fin, k_unit, k_inv = head_norm(k_raw, k_norm, cos_t, sin_t)
        q_fin = q_fin.reshape(n_batch, seq_loc, kv_heads, groups, head_dim)

        stat_shape = (n_batch, kv_heads, groups, seq_loc)
        init_stats = (jnp.full(stat_shape, NEG_BIG, jnp.float32), jnp.zeros(stat_shape, jnp.float32), jnp.zeros(stat_shape + (head_dim,), jnp.float32))
        run_stats = attend_block(init_stats, q_fin, k_fin, v_loc, pos_loc, pos_loc, score_scale)

        def fwd_step(step_idx, loop_state):
            k_blk, v_blk, k_pos, carried = loop_state
            k_blk, v_blk, k_pos = lax.ppermute((k_blk, v_blk, k_pos), 'cp', next_hop)
            return k_blk, v_blk, k_pos, attend_block(carried, q_fin, k_blk, v_blk, pos_loc, k_pos, score_scale)

        final_state = lax.fori_loop(0, n_cp - 1, fwd_step, (k_fin, v_loc, pos_loc, run_stats))
        run_max, run_sum, run_acc = final_state[3]
        out_f32 = run_acc / run_sum[..., None]
        log_norm = run_max + jnp.log(run_sum)
        out_bf = out_f32.astype(jnp.bfloat16)
        wo_split = w_o.reshape(kv_heads, groups, head_dim, model_dim)
        attn = lax.psum(jnp.einsum('bkgqd,kgdm->bqm', out_bf, wo_split, preferred_element_type=jnp.float32), 'tp')
        attn_unit, attn_inv = rms_unit(attn)
        output = (x_f32 + attn_unit * (1.0 + w_post)).astype(jnp.bfloat16)

        grad_y = cotangent.astype(jnp.float32)
        d_post = lax.psum(jnp.sum(grad_y * attn_unit, axis=(0, 1)), 'cp')
        d_attn = rms_unit_back(grad_y * (1.0 + w_post), attn_unit, attn_inv).astype(jnp.bfloat16)
        d_wo = lax.psum(jnp.einsum('bkgqd,bqm->kgdm', out_bf, d_attn, preferred_element_type=jnp.float32), 'cp').reshape(q_heads * head_dim, model_dim)
        d_out = jnp.einsum('bqm,kgdm->bkgqd', d_attn, wo_split, preferred_element_type=jnp.float32)
        row_delta = jnp.sum(d_out * out_f32, axis=-1)
        d_out_bf = d_out.astype(jnp.bfloat16)

        dq_first, dk_first, dv_first = grad_block(q_fin, d_out_bf, log_norm, row_delta, pos_loc, k_fin, v_loc, pos_loc, score_scale)

        def bwd_step(step_idx, loop_state):
            k_blk, v_blk, k_pos, dk_run, dv_run, dq_run = loop_state
            k_blk, v_blk, k_pos, dk_run, dv_run = lax.ppermute((k_blk, v_blk, k_pos, dk_run, dv_run), 'cp', next_hop)
            grad_q, grad_k, grad_v = grad_block(q_fin, d_out_bf, log_norm, row_delta, pos_loc, k_blk, v_blk, k_pos, score_scale)
            return k_blk, v_blk, k_pos, dk_run + grad_k, dv_run + grad_v, dq_run + grad_q

        back_state = lax.fori_loop(0, n_cp - 1, bwd_step, (k_fin, v_loc, pos_loc, dk_first, dv_first, dq_first))
        dk_home, dv_home = lax.ppermute((back_state[3], back_state[4]), 'cp', next_hop)
        dq_all = back_state[5].reshape(n_batch, seq_loc, q_heads, head_dim)

        dq_raw, dq_gain = head_norm_back(dq_all, q_norm, q_unit, q_inv, cos_t, sin_t)
        dk_raw, dk_gain = head_norm_back(dk_home, k_norm, k_unit, k_inv, cos_t, sin_t)
        dq_bf = dq_raw.reshape(n_batch, seq_loc, q_heads * head_dim).astype(jnp.bfloat16)
        dk_bf = dk_raw.reshape(n_batch, seq_loc, kv_heads * head_dim).astype(jnp.bfloat16)
        dv_bf = dv_home.reshape(n_batch, seq_loc, kv_heads * head_dim).astype(jnp.bfloat16)
        d_wq = lax.psum(jnp.einsum('bsd,bsh->dh', normed, dq_bf, preferred_element_type=jnp.float32), 'cp')
        d_wk = lax.psum(jnp.einsum('bsd,bsh->dh', normed, dk_bf, preferred_element_type=jnp.float32), 'cp')
        d_wv = lax.psum(jnp.einsum('bsd,bsh->dh', normed, dv_bf, preferred_element_type=jnp.float32), 'cp')
        d_normed = lax.psum(jnp.einsum('bsh,dh->bsd', dq_bf, w_q, preferred_element_type=jnp.float32) + jnp.einsum('bsh,dh->bsd', dk_bf, w_k, preferred_element_type=jnp.float32) + jnp.einsum('bsh,dh->bsd', dv_bf, w_v, preferred_element_type=jnp.float32), 'tp')
        d_qnorm = lax.psum(dq_gain, ('tp', 'cp'))
        d_knorm = lax.psum(dk_gain, ('tp', 'cp'))
        d_pre = lax.psum(jnp.sum(d_normed * x_unit, axis=(0, 1)), 'cp')
        d_hidden = (grad_y + rms_unit_back(d_normed * (1.0 + w_pre), x_unit, x_inv)).astype(jnp.bfloat16)
        return output, d_hidden, d_wq, d_wk, d_wv, d_wo, d_pre, d_post, d_qnorm, d_knorm

    specs_in = (P('dp', 'cp', None), P('dp', 'cp', None), P(('dp', 'cp')), P(None, 'tp'), P(None, 'tp'), P(None, 'tp'), P('tp', None), P(None), P(None), P(None), P(None))
    specs_out = (P('dp', 'cp', None), P('dp', 'cp', None), P('dp', 'tp'), P('dp', 'tp'), P('dp', 'tp'), P(('dp', 'tp'), None), P('dp'), P('dp'), P('dp'), P('dp'))
    return jax.shard_map(per_device, mesh=mesh, in_specs=specs_in, out_specs=specs_out, check_vma=False)
```

profile of v0, /device:TPU:0, one launch (start us, length us, event | category | flops | bytes accessed | tf_op | source)
XLA Modules:
  0.0 5701.4 jit_solution(13005662809528821658)
XLA Ops:
  94.2 43.3 convert_convert_fusion
  190.5 30.2 fusion.29
  249.6 35.0 broadcast_add_fusion
  284.6 409.2 %while.40 = (s32[]{:T(128)}, bf16[2,768,8,128]{3,1,2,0:T(8,128)(2,1)}, bf16[2,768,8,128]{3,1,2,0:T(8,128)(2,1)}, s32[768]{0:T(1024)S(1)}, f32[2,8,2,768]{3,2,1,0...) while((s32[]{:T(128)}, ...), condition=%wide.region_8.9_spmd, body=%wide.region_5.8_spmd.sunk | while | flops 9878224896 | bytes 305946816 | solution.py:110
  288.1 34.3 collective-permute-done.2
  322.8 30.3 fusion.169
  385.0 36.7 multiply_add_fusion.7
  424.2 34.3 collective-permute-done.2
  458.9 30.3 fusion.169
  521.1 36.7 multiply_add_fusion.7
  560.2 34.3 collective-permute-done.2
  595.0 30.3 fusion.169
  657.2 36.7 multiply_add_fusion.7
  706.5 44.2 convolution_bitcast_fusion.1
  784.5 688.7 %all-reduce.8.cloned.1.call-done = f32[2,768,5376]{2,1,0:T(8,128)} async-done(((f32[2,768,5376]{2,1,0:T(8,128)}), f32[2,768,5376]{2,1,0:T(8,128)}) %all-reduce.8.cloned.1.call-update) | async-done | bytes 33030160 | tf_op jit(solution)/shard_map/psum | solution.py:116
  1506.8 33.2 fusion.51
  1540.0 44.4 fusion.70
  1584.5 30.7 fusion.100
  1615.2 45.1 multiply_convert_fusion.1
  1736.1 719.1 %while.41 = (s32[]{:T(128)}, bf16[2,768,8,128]{3,1,2,0:T(8,128)(2,1)}, bf16[2,768,8,128]{3,1,2,0:T(8,128)(2,1)}, s32[768]{0:T(1024)S(1)}, f32[2,768,8,128]{3,1,2...) while((s32[]{:T(128)}, ...), condition=%wide.region_14.15_spmd, body=%wide.region_13.14_spmd.sunk | while | flops 24373690368 | bytes 518787552 | solution.py:136
  1740.1 34.5 collective-permute-done.5
  1777.1 28.8 fusion.181
  1808.3 43.7 multiply_convert_fusion.4
  1902.9 40.1 collective-permute-done.7
  1943.1 32.9 bitcast_add_fusion.7
  1979.6 34.5 collective-permute-done.5
  2016.6 28.8 fusion.181
  2047.8 43.7 multiply_convert_fusion.4
  2142.5 40.1 collective-permute-done.7
  2182.6 32.9 bitcast_add_fusion.7
  2219.1 34.5 collective-permute-done.5
  2256.1 28.8 fusion.181
  2287.3 43.7 multiply_convert_fusion.4
  2381.9 40.1 collective-permute-done.7
  2422.1 32.9 bitcast_add_fusion.7
  2475.6 28.5 multiply_add_fusion.2
  2583.9 40.0 fusion.61
  2682.6 41.8 add_add_fusion
  2725.3 48.8 fusion.65
  2774.1 31.3 copy.264
  2806.1 43.8 convolution_bitcast_fusion
  2875.1 31.8 convolution_bitcast_fusion.3
  2930.6 516.0 %all-reduce.10.cloned.1.call-done = f32[2,768,5376]{2,1,0:T(8,128)} async-done(((f32[2,768,5376]{2,1,0:T(8,128)}), f32[2,768,5376]{2,1,0:T(8,128)}) %all-reduce.10.cloned.1.call-update) | async-done | bytes 33030160 | tf_op jit(solution)/shard_map/psum | solution.py:148
  3478.3 27.6 fusion.59
  3505.9 665.2 %all-reduce.12.cloned.1.call-done = f32[2048,5376]{1,0:T(8,128)} async-done(((f32[2048,5376]{1,0:T(8,128)}), f32[2048,5376]{1,0:T(8,128)}) %all-reduce.12.cloned.1.call-update) | async-done | bytes 44040208 | tf_op jit(solution)/shard_map/psum | solution.py:123
  4171.1 1432.0 %all-reduce.14.cloned.1.call-done = (f32[5376,2048]{1,0:T(8,128)}, f32[5376,1024]{1,0:T(8,128)}, f32[5376,1024]{1,0:T(8,128)}) async-done(((f32[5376,2048]{1,0:T(8,128)}, f32[5376,1024]{1,0:T(8,128)}, f32[5376,1024]{1,0:T(8,128)}), (f32[5376,2048]{1,0:T(8,128)}, f32[5376,1024]{1,0:T(8,128)}, f32[5376,1024]{1,0:T(8,128)})) %all-reduce.14.cloned.1.call-update) | async-done | bytes 88080400 | tf_op jit(solution)/shard_map/psum | solution.py:145
  5603.1 32.0 copy.358
  5664.2 30.5 copy.361
  (329 shorter events, 878.1 us)
Async XLA Ops:
  7.2 1466.1 %all-reduce.8.cloned.1.call-start = ((), (), s32[]{:S(2)}) async-start(), calls=%async_computation | async-start | bytes 66060288 | tf_op jit(solution)/shard_map/psum | solution.py:116
  21.7 72.5 %copy-start.34 = (f32[2,768]{1,0:T(2,128)}, f32[2,768]{1,0:T(2,128)S(1)}, u32[]{:S(2)}) copy-start(f32[2,768]{1,0:T(2,128)S(1)} %add_rsqrt_fusion.3) | copy-start | bytes 18436
  51.4 116.1 %copy-start.14 = (f32[768,64]{1,0:T(8,128)}, f32[768,64]{1,0:T(8,128)S(1)}, u32[]{:S(2)}) copy-start(f32[768,64]{1,0:T(8,128)S(1)} %get-tuple-element.334) | copy-start | bytes 589828
  94.2 63.8 %copy-start.44 = (f32[128]{0:T(128)}, f32[128]{0:T(128)S(1)}, u32[]{:S(2)}) copy-start(f32[128]{0:T(128)S(1)} %broadcast_add_fusion.3) | copy-start | bytes 1540
  284.6 38.2 collective-permute-start
  285.5 36.9 collective-permute-start.2
  288.1 93.1 %collective-permute-start.1 = (bf16[2,768,8,128]{3,1,2,0:T(8,128)(2,1)}, bf16[2,768,8,128]{3,1,2,0:T(8,128)(2,1)}, u32[]{:S(2)}, u32[]{:S(2)}) collective-permute-start(bf16[2,768,8,128]{3,1,2,0:T(8,128)(2,1)} %get-tuple-element.494), channel_id=1, source_target_pairs={{0,1},{1,2},{2,3},{3,0},{4,5},{5,6},{6,7},{7,4}} | collective-permute-start | bytes 9437192 | tf_op jit(solution)/shard_map/while/body/eval_jaxpr/ppermute | solution.py:107
  421.7 37.1 collective-permute-start
  421.7 36.7 collective-permute-start.2
  424.2 93.1 %collective-permute-start.1 = (bf16[2,768,8,128]{3,1,2,0:T(8,128)(2,1)}, bf16[2,768,8,128]{3,1,2,0:T(8,128)(2,1)}, u32[]{:S(2)}, u32[]{:S(2)}) collective-permute-start(bf16[2,768,8,128]{3,1,2,0:T(8,128)(2,1)} %get-tuple-element.494), channel_id=1, source_target_pairs={{0,1},{1,2},{2,3},{3,0},{4,5},{5,6},{6,7},{7,4}} | collective-permute-start | bytes 9437192 | tf_op jit(solution)/shard_map/while/body/eval_jaxpr/ppermute | solution.py:107
  557.8 37.1 collective-permute-start
  557.8 36.7 collective-permute-start.2
  560.2 93.1 %collective-permute-start.1 = (bf16[2,768,8,128]{3,1,2,0:T(8,128)(2,1)}, bf16[2,768,8,128]{3,1,2,0:T(8,128)(2,1)}, u32[]{:S(2)}, u32[]{:S(2)}) collective-permute-start(bf16[2,768,8,128]{3,1,2,0:T(8,128)(2,1)} %get-tuple-element.494), channel_id=1, source_target_pairs={{0,1},{1,2},{2,3},{3,0},{4,5},{5,6},{6,7},{7,4}} | collective-permute-start | bytes 9437192 | tf_op jit(solution)/shard_map/while/body/eval_jaxpr/ppermute | solution.py:107
  693.9 846.2 %copy-start.21 = (f32[2,8,2,768]{3,2,1,0:T(2,128)}, f32[2,8,2,768]{3,2,1,0:T(2,128)S(1)}, u32[]{:S(2)}) copy-start(f32[2,8,2,768]{3,2,1,0:T(2,128)S(1)} %get-tuple-element.124) | copy-start | bytes 294916
  750.7 2695.8 %all-reduce.10.cloned.1.call-start = ((), (), s32[]{:S(2)}) async-start(), calls=%async_computation.1 | async-start | bytes 66060288 | tf_op jit(solution)/shard_map/psum | solution.py:148
  1737.8 39.2 collective-permute-start.3
  1737.8 36.7 collective-permute-start.5
  1739.4 68.9 %collective-permute-start.4 = (bf16[2,768,8,128]{3,1,2,0:T(8,128)(2,1)}, bf16[2,768,8,128]{3,1,2,0:T(8,128)(2,1)}, u32[]{:S(2)}, u32[]{:S(2)}) collective-permute-start(bf16[2,768,8,128]{3,1,2,0:T(8,128)(2,1)} %get-tuple-element.527), channel_id=1, source_target_pairs={{0,1},{1,2},{2,3},{3,0},{4,5},{5,6},{6,7},{7,4}} | collective-permute-start | bytes 9437192 | tf_op jit(solution)/shard_map/while/body/eval_jaxpr/ppermute | solution.py:132
  1739.4 140.9 %collective-permute-start.6 = (f32[2,768,8,128]{3,1,2,0:T(8,128)}, f32[2,768,8,128]{3,1,2,0:T(8,128)}, u32[]{:S(2)}, u32[]{:S(2)}) collective-permute-start(f32[2,768,8,128]{3,1,2,0:T(8,128)} %get-tuple-element.529), channel_id=1, source_target_pairs={{0,1},{1,2},{2,3},{3,0},{4,5},{5,6},{6,7},{7,4}} | collective-permute-start | bytes 18874376 | tf_op jit(solution)/shard_map/while/body/eval_jaxpr/ppermute | solution.py:132
  1740.1 203.0 %collective-permute-start.7 = (f32[2,768,8,128]{3,1,2,0:T(8,128)}, f32[2,768,8,128]{3,1,2,0:T(8,128)}, u32[]{:S(2)}, u32[]{:S(2)}) collective-permute-start(f32[2,768,8,128]{3,1,2,0:T(8,128)} %get-tuple-element.530), channel_id=1, source_target_pairs={{0,1},{1,2},{2,3},{3,0},{4,5},{5,6},{6,7},{7,4}} | collective-permute-start | bytes 18874376 | tf_op jit(solution)/shard_map/while/body/eval_jaxpr/ppermute | solution.py:132
  1880.3 62.8 %copy-start.8 = (pred[768,768]{0,1:T(8,128)(4,1)S(1)}, pred[768,768]{0,1:T(8,128)(4,1)}, u32[]{:S(2)}) copy-start(pred[768,768]{0,1:T(8,128)(4,1)} %broadcast_compare_fusion.6) | copy-start | bytes 1769476 | tf_op jit(solution)/shard_map/while
  1880.3 62.8 %copy-start.33 = (f32[2,8,2,768]{3,2,1,0:T(2,128)S(1)}, f32[2,8,2,768]{3,2,1,0:T(2,128)}, u32[]{:S(2)}) copy-start(f32[2,8,2,768]{3,2,1,0:T(2,128)} %copy-done.32) | copy-start | bytes 294916 | tf_op jit(solution)/shard_map/while
  1902.9 73.1 %copy-start.49 = (s32[768]{0:T(1024)S(1)}, s32[768]{0:T(1024)}, u32[]{:S(2)}) copy-start(s32[768]{0:T(1024)} %copy.347) | copy-start | bytes 9220 | tf_op jit(solution)/shard_map/while
  1902.9 73.1 %copy-start.52 = (f32[2,8,2,768]{3,2,1,0:T(2,128)S(1)}, f32[2,8,2,768]{3,2,1,0:T(2,128)}, u32[]{:S(2)}) copy-start(f32[2,8,2,768]{3,2,1,0:T(2,128)} %copy-done.51) | copy-start | bytes 294916 | tf_op jit(solution)/shard_map/while
  1977.3 39.2 collective-permute-start.3
  1977.3 36.7 collective-permute-start.5
  1978.9 68.9 %collective-permute-start.4 = (bf16[2,768,8,128]{3,1,2,0:T(8,128)(2,1)}, bf16[2,768,8,128]{3,1,2,0:T(8,128)(2,1)}, u32[]{:S(2)}, u32[]{:S(2)}) collective-permute-start(bf16[2,768,8,128]{3,1,2,0:T(8,128)(2,1)} %get-tuple-element.527), channel_id=1, source_target_pairs={{0,1},{1,2},{2,3},{3,0},{4,5},{5,6},{6,7},{7,4}} | collective-permute-start | bytes 9437192 | tf_op jit(solution)/shard_map/while/body/eval_jaxpr/ppermute | solution.py:132
  1978.9 140.9 %collective-permute-start.6 = (f32[2,768,8,128]{3,1,2,0:T(8,128)}, f32[2,768,8,128]{3,1,2,0:T(8,128)}, u32[]{:S(2)}, u32[]{:S(2)}) collective-permute-start(f32[2,768,8,128]{3,1,2,0:T(8,128)} %get-tuple-element.529), channel_id=1, source_target_pairs={{0,1},{1,2},{2,3},{3,0},{4,5},{5,6},{6,7},{7,4}} | collective-permute-start | bytes 18874376 | tf_op jit(solution)/shard_map/while/body/eval_jaxpr/ppermute | solution.py:132
  1979.6 203.0 %collective-permute-start.7 = (f32[2,768,8,128]{3,1,2,0:T(8,128)}, f32[2,768,8,128]{3,1,2,0:T(8,128)}, u32[]{:S(2)}, u32[]{:S(2)}) collective-permute-start(f32[2,768,8,128]{3,1,2,0:T(8,128)} %get-tuple-element.530), channel_id=1, source_target_pairs={{0,1},{1,2},{2,3},{3,0},{4,5},{5,6},{6,7},{7,4}} | collective-permute-start | bytes 18874376 | tf_op jit(solution)/shard_map/while/body/eval_jaxpr/ppermute | solution.py:132
  2142.4 73.1 %copy-start.49 = (s32[768]{0:T(1024)S(1)}, s32[768]{0:T(1024)}, u32[]{:S(2)}) copy-start(s32[768]{0:T(1024)} %copy.347) | copy-start | bytes 9220 | tf_op jit(solution)/shard_map/while
  2142.5 73.1 %copy-start.52 = (f32[2,8,2,768]{3,2,1,0:T(2,128)S(1)}, f32[2,8,2,768]{3,2,1,0:T(2,128)}, u32[]{:S(2)}) copy-start(f32[2,8,2,768]{3,2,1,0:T(2,128)} %copy-done.51) | copy-start | bytes 294916 | tf_op jit(solution)/shard_map/while
  2216.8 39.2 collective-permute-start.3
  2216.8 36.7 collective-permute-start.5
  2218.4 68.9 %collective-permute-start.4 = (bf16[2,768,8,128]{3,1,2,0:T(8,128)(2,1)}, bf16[2,768,8,128]{3,1,2,0:T(8,128)(2,1)}, u32[]{:S(2)}, u32[]{:S(2)}) collective-permute-start(bf16[2,768,8,128]{3,1,2,0:T(8,128)(2,1)} %get-tuple-element.527), channel_id=1, source_target_pairs={{0,1},{1,2},{2,3},{3,0},{4,5},{5,6},{6,7},{7,4}} | collective-permute-start | bytes 9437192 | tf_op jit(solution)/shard_map/while/body/eval_jaxpr/ppermute | solution.py:132
  2218.4 140.9 %collective-permute-start.6 = (f32[2,768,8,128]{3,1,2,0:T(8,128)}, f32[2,768,8,128]{3,1,2,0:T(8,128)}, u32[]{:S(2)}, u32[]{:S(2)}) collective-permute-start(f32[2,768,8,128]{3,1,2,0:T(8,128)} %get-tuple-element.529), channel_id=1, source_target_pairs={{0,1},{1,2},{2,3},{3,0},{4,5},{5,6},{6,7},{7,4}} | collective-permute-start | bytes 18874376 | tf_op jit(solution)/shard_map/while/body/eval_jaxpr/ppermute | solution.py:132
  2219.1 203.0 %collective-permute-start.7 = (f32[2,768,8,128]{3,1,2,0:T(8,128)}, f32[2,768,8,128]{3,1,2,0:T(8,128)}, u32[]{:S(2)}, u32[]{:S(2)}) collective-permute-start(f32[2,768,8,128]{3,1,2,0:T(8,128)} %get-tuple-element.530), channel_id=1, source_target_pairs={{0,1},{1,2},{2,3},{3,0},{4,5},{5,6},{6,7},{7,4}} | collective-permute-start | bytes 18874376 | tf_op jit(solution)/shard_map/while/body/eval_jaxpr/ppermute | solution.py:132
  2359.3 62.8 %copy-start.8 = (pred[768,768]{0,1:T(8,128)(4,1)S(1)}, pred[768,768]{0,1:T(8,128)(4,1)}, u32[]{:S(2)}) copy-start(pred[768,768]{0,1:T(8,128)(4,1)} %broadcast_compare_fusion.6) | copy-start | bytes 1769476 | tf_op jit(solution)/shard_map/while
  2359.3 62.8 %copy-start.33 = (f32[2,8,2,768]{3,2,1,0:T(2,128)S(1)}, f32[2,8,2,768]{3,2,1,0:T(2,128)}, u32[]{:S(2)}) copy-start(f32[2,8,2,768]{3,2,1,0:T(2,128)} %copy-done.32) | copy-start | bytes 294916 | tf_op jit(solution)/shard_map/while
  2381.9 73.1 %copy-start.49 = (s32[768]{0:T(1024)S(1)}, s32[768]{0:T(1024)}, u32[]{:S(2)}) copy-start(s32[768]{0:T(1024)} %copy.347) | copy-start | bytes 9220 | tf_op jit(solution)/shard_map/while
  2381.9 73.1 %copy-start.52 = (f32[2,8,2,768]{3,2,1,0:T(2,128)S(1)}, f32[2,8,2,768]{3,2,1,0:T(2,128)}, u32[]{:S(2)}) copy-start(f32[2,8,2,768]{3,2,1,0:T(2,128)} %copy-done.51) | copy-start | bytes 294916 | tf_op jit(solution)/shard_map/while
  2556.3 70.4 %collective-permute-start.8 = (f32[2,768,8,128]{3,1,2,0:T(8,128)}, f32[2,768,8,128]{3,1,2,0:T(8,128)S(1)}, u32[]{:S(2)}, u32[]{:S(2)}) collective-permute-start(f32[2,768,8,128]{3,1,2,0:T(8,128)} %get-tuple-element.127), channel_id=1, source_target_pairs={{0,1},{1,2},{2,3},{3,0},{4,5},{5,6},{6,7},{7,4}} | collective-permute-start | bytes 18874376 | tf_op jit(solution)/shard_map/ppermute | solution.py:137
  2561.3 121.3 %collective-permute-start.9 = (bf16[2,768,8,128]{3,1,2,0:T(8,128)(2,1)}, bf16[2,768,8,128]{3,1,2,0:T(8,128)(2,1)}, u32[]{:S(2)}, u32[]{:S(2)}) collective-permute-start(bf16[2,768,8,128]{3,1,2,0:T(8,128)(2,1)} %convert.33), channel_id=1, source_target_pairs={{0,1},{1,2},{2,3},{3,0},{4,5},{5,6},{6,7},{7,4}} | collective-permute-start | bytes 9437192 | tf_op jit(solution)/shard_map/ppermute | solution.py:137
  2724.4 1446.7 %all-reduce.12.cloned.1.call-start = ((), (), s32[]{:S(2)}) async-start(), calls=%async_computation.2 | async-start | bytes 88080384 | tf_op jit(solution)/shard_map/psum | solution.py:123
  2805.4 2797.6 %all-reduce.14.cloned.1.call-start = ((), (), s32[]{:S(2)}) async-start(), calls=%async_computation.3 | async-start | bytes 176160768 | tf_op jit(solution)/shard_map/psum | solution.py:145
  2806.1 68.9 %slice-start.4 = ((s8[16515072]{0:T(1024)(128)(4,1)}), s8[4194304]{0:T(1024)(128)(4,1)S(1)}, s32[]{:S(2)}) async-start(s8[16515072]{0:T(1024)(128)(4,1)} %bitcast.365), calls=%async_computation.8 | async-start | bytes 8388608
  2806.1 68.9 %slice-start.5 = ((s8[16515072]{0:T(1024)(128)(4,1)}), s8[4194304]{0:T(1024)(128)(4,1)S(1)}, s32[]{:S(2)}) async-start(s8[16515072]{0:T(1024)(128)(4,1)} %bitcast.365), calls=%async_computation.9 | async-start | bytes 8388608
  2806.1 68.9 %slice-start.6 = ((s8[16515072]{0:T(1024)(128)(4,1)}), s8[4194304]{0:T(1024)(128)(4,1)S(1)}, s32[]{:S(2)}) async-start(s8[16515072]{0:T(1024)(128)(4,1)} %bitcast.365), calls=%async_computation.10 | async-start | bytes 8388608
  2930.6 534.3 %copy-start.31 = (f32[5376]{0:T(1024)S(1)}, f32[5376]{0:T(1024)}, u32[]{:S(2)}) copy-start(f32[5376]{0:T(1024)} %get-tuple-element.255) | copy-start | bytes 64516
  (58 other events, 894.9 us)
Sparse Core Ops, SparseCore 0:
  750.9 722.3 all-reduce.7
  2724.5 721.9 all-reduce.9
  3449.6 721.4 all-reduce.11
  4174.2 1428.7 all-reduce.13
where the time goes:
time: 5710 us; the launch traced here: 5700 us
  waiting for transfers between devices  3640 us (64%)
  matrix products  1270 us (22%)
  local copies, waits for them, and re-layouts  369 us (6%)
  other arithmetic  358 us (6%)
    psum x1, waiting for transfers between devices, per_device(): lax.psum(jnp.einsum('bsd,bsh->dh', normed, dq_bf, preferred_element_type=...  1430 us
    psum x1, waiting for transfers between devices, per_device(): lax.psum(jnp.einsum('bkgqd,kgdm->bqm', out_bf, wo_split, preferred_elemen...  689 us
    psum x1, waiting for transfers between devices, per_device(): lax.psum(jnp.einsum('bkgqd,bqm->kgdm', out_bf, d_attn, preferred_element_...  665 us
    psum x1, waiting for transfers between devices, per_device(): lax.psum(jnp.einsum('bsh,dh->bsd', dq_bf, w_q, preferred_element_type=jnp...  516 us
    ppermute x15, waiting for transfers between devices, bwd_step(): lax.ppermute((k_blk, v_blk, k_pos, dk_run, dv_run), 'cp', next_hop)  231 us
    dot_general x4, matrix products, grad_block(): jnp.einsum('bkgqd,bskd->bkgqs', d_out, v_blk, preferred_element_type=jnp....  176 us
    dot_general x4, matrix products, attend_block(): jnp.einsum('bkgqs,bskd->bkgqd', attn_prob.astype(jnp.bfloat16), v_blk, pr...  145 us
    unnamed x128, local copies, waits for them, and re-layouts  132 us
  transfers between devices with their start and end apart: 30, of which 17 were waited for; matrix products, arithmetic and copies ran while one was open for 16% of the time, Pallas kernels for 0%

commit v1 on v0

v1 whole, which is shorter than its diff:
```python
import functools

import jax
import jax.numpy as jnp
from jax import lax
from jax.experimental import pallas as pl
from jax.experimental.pallas import tpu as pltpu
from jax.sharding import PartitionSpec as P

EPS = 1e-6
ROPE_BASE = 1000000.0
ROPE_SCALE = 8.0
NEG_BIG = -1e30
LOG2E = 1.4426950408889634
VMEM_CAP = 60 * 1024 * 1024
F32 = jnp.float32
BF16 = jnp.bfloat16

S_DEV, S_TP, S_CORE, S_X, S_PEER, S_BLOCK = 0, 1, 2, 3, 4, 8

NN = (((1,), (0,)), ((), ()))
NT = (((1,), (1,)), ((), ()))
TN = (((0,), (0,)), ((), ()))


def mm(lhs, rhs, dims=NN):
    return lax.dot_general(lhs, rhs, dims, preferred_element_type=F32)


def params(n_grid, vmem=VMEM_CAP):
    sem = ("arbitrary",) * n_grid if n_grid else None
    return pltpu.CompilerParams(dimension_semantics=sem, vmem_limit_bytes=vmem)


def cost(flops, nbytes, trans=0):
    return pl.CostEstimate(flops=int(flops), bytes_accessed=int(nbytes), transcendentals=int(trans))


def qkv_kernel(s_ref, x_ref, wpre_ref, wq_ref, wk_ref, wv_ref, normed_ref, *outs):
    peer = pl.program_id(1)
    rows = normed_ref.shape[0]
    qw, kw = wq_ref.shape[1], wk_ref.shape[1]

    @pl.when(peer == 0)
    def _():
        gain = 1.0 + wpre_ref[...]

        def chunk(step, carry):
            here = pl.ds(pl.multiple_of(step * 16, 16), 16)
            xf = x_ref[0, here, :].astype(F32)
            inv = lax.rsqrt(jnp.mean(xf * xf, axis=-1, keepdims=True) + EPS)
            normed_ref[here, :] = (xf * inv * gain).astype(BF16)
            return carry

        lax.fori_loop(0, rows // 16, chunk, 0)

    normed = normed_ref[...]
    for rel in range(4):
        @pl.when(peer == rel)
        def _(out=outs[rel]):
            out[:, :qw] = mm(normed, wq_ref[...]).astype(BF16)
            out[:, qw:qw + kw] = mm(normed, wk_ref[...]).astype(BF16)
            out[:, qw + kw:] = mm(normed, wv_ref[...]).astype(BF16)


def project(table, hidden, w_pre, w_q, w_k, w_v, batch, n_blocks):
    _, seq, width = hidden.shape
    qw, kw = w_q.shape[1] // n_blocks, w_k.shape[1] // n_blocks
    tile = 384
    row = lambda t, r, s: (t, 0)
    col = lambda t, r, s: (0, s[S_BLOCK + r])
    block = qw + 2 * kw
    return pl.pallas_call(
        qkv_kernel,
        grid_spec=pltpu.PrefetchScalarGridSpec(
            num_scalar_prefetch=1,
            grid=(seq // tile, n_blocks),
            in_specs=[
                pl.BlockSpec((1, tile, width), lambda t, r, s: (batch, t, 0)),
                pl.BlockSpec((1, width), lambda t, r, s: (0, 0)),
                pl.BlockSpec((width, qw), col),
                pl.BlockSpec((width, kw), col),
                pl.BlockSpec((width, kw), col),
            ],
            out_specs=[pl.BlockSpec((tile, width), row)] + [pl.BlockSpec((tile, block), row)] * n_blocks,
        ),
        out_shape=[jax.ShapeDtypeStruct((seq, width), BF16)] + [jax.ShapeDtypeStruct((seq, block), BF16)] * n_blocks,
        compiler_params=params(2),
        cost_estimate=cost(2 * seq * width * block * n_blocks, 4 * seq * width + 4 * width * block * n_blocks),
        name="qkv",
    )(table, hidden, w_pre, w_q, w_k, w_v)


def rope_fwd(vals, cos2, sin2):
    return vals * cos2 + pltpu.roll(vals, vals.shape[-1] // 2, 1) * sin2


def rope_bwd(grads, cos2, sin2):
    return grads * cos2 - pltpu.roll(grads, grads.shape[-1] // 2, 1) * sin2


def unit_of(raw):
    vals = raw.astype(F32)
    inv = lax.rsqrt(jnp.mean(vals * vals, axis=-1, keepdims=True) + EPS)
    return vals * inv, inv


def final_head(raw, gain, cos2, sin2):
    unit, _ = unit_of(raw)
    return rope_fwd(unit * gain, cos2, sin2).astype(BF16)


def gather_pieces(s_ref, srcs, dst, sems, piece, n_dev):
    copies = []
    for rel, src in enumerate(srcs):
        peer = s_ref[S_PEER + rel]
        for half in range(2):
            where = peer if half == 0 else 2 * n_dev - 1 - peer
            copies.append(pltpu.make_async_copy(
                src.at[pl.ds(half * piece, piece)],
                dst.at[pl.ds(pl.multiple_of(where * piece, piece), piece)],
                sems.at[2 * rel + half]))
    return copies


def slot_of(piece_idx, n_dev):
    return jnp.where(piece_idx < n_dev, 2 * piece_idx, 4 * n_dev - 1 - 2 * piece_idx)


def causal_t(piece, groups):
    keys = lax.broadcasted_iota(jnp.int32, (piece, piece), 0)
    queries = lax.broadcasted_iota(jnp.int32, (piece, piece), 1)
    return jnp.concatenate([keys <= queries] * groups, axis=1)


def attend_kernel(s_ref, a0, a1, a2, a3, cos_ref, sin_ref, qg_ref, kg_ref, out_ref, lse_ref,
                  raw, kf, vt, qf, m_ref, l_ref, acc, sems, *, dim, kv, groups, piece, n_dev):
    qw, kw = kv * groups * dim, kv * dim
    n_piece = 2 * n_dev
    scale = dim ** -0.5 * LOG2E
    copies = gather_pieces(s_ref, (a0, a1, a2, a3), raw, sems, piece, n_dev)
    for copy in copies:
        copy.start()
    for copy in copies:
        copy.wait()
    k_gain = 1.0 + kg_ref[...]
    q_gain = 1.0 + qg_ref[...]

    def rows_of(idx):
        return pl.ds(pl.multiple_of(idx * piece, piece), piece)

    def prepare(idx, carry):
        here = rows_of(idx)
        cos2, sin2 = cos_ref[here, :], sin_ref[here, :]
        for h in range(kv):
            kf[h, here, :] = final_head(raw[here, qw + h * dim:qw + (h + 1) * dim], k_gain, cos2, sin2)
            vals = raw[here, qw + kw + h * dim:qw + kw + (h + 1) * dim]
            vt[h, :, here] = vals.astype(F32).T.astype(BF16)
        return carry

    lax.fori_loop(0, n_piece, prepare, 0)

    def block(idx, h, first, mask):
        here = rows_of(idx)
        sc = mm(kf[h, here, :], qf[h], NT) * scale
        if mask is not None:
            sc = jnp.where(mask, sc, NEG_BIG)
        top = jnp.max(sc, axis=0, keepdims=True)
        if first:
            new = top
        else:
            old = m_ref[h]
            new = jnp.maximum(old, top)
        prob = jnp.exp2(sc - new)
        tot = jnp.sum(prob, axis=0, keepdims=True)
        part = mm(vt[h, :, here], prob.astype(BF16))
        m_ref[h] = new
        if first:
            l_ref[h] = tot
            acc[h] = part
        else:
            fac = jnp.exp2(old - new)
            l_ref[h] = l_ref[h] * fac + tot
            acc[h] = acc[h] * fac + part

    def query_piece(p, carry):
        here = rows_of(p)
        cos2, sin2 = cos_ref[here, :], sin_ref[here, :]
        for h in range(kv):
            for g in range(groups):
                head = h * groups + g
                qf[h, g * piece:(g + 1) * piece, :] = final_head(
                    raw[here, head * dim:(head + 1) * dim], q_gain, cos2, sin2)
        mask = causal_t(piece, groups)
        for h in range(kv):
            block(p, h, True, mask)

        def inner(j, c):
            for h in range(kv):
                block(j, h, False, None)
            return c

        lax.fori_loop(0, p, inner, 0)
        there = rows_of(slot_of(p, n_dev))
        for h in range(kv):
            total = l_ref[h]
            o_t = acc[h] / total
            lse = m_ref[h] + jnp.log2(total)
            for g in range(groups):
                head = h * groups + g
                cols = slice(g * piece, (g + 1) * piece)
                out_ref[there, head * dim:(head + 1) * dim] = o_t[:, cols].T.astype(BF16)
                lse_ref[head:head + 1, here] = lse[:, cols]
        return carry

    lax.fori_loop(0, n_piece, query_piece, 0)


def attend(table, blocks, cos2, sin2, q_norm, k_norm, dim, kv, groups):
    seq = blocks[0].shape[0]
    n_dev = len(blocks)
    width = blocks[0].shape[1]
    total, piece, heads = seq * n_dev, seq // 2, kv * groups
    vm = pl.BlockSpec(memory_space=pltpu.VMEM)
    hbm = pl.BlockSpec(memory_space=pl.ANY)
    flops = 4 * heads * dim * total * total * 9 / 16
    return pl.pallas_call(
        functools.partial(attend_kernel, dim=dim, kv=kv, groups=groups, piece=piece, n_dev=n_dev),
        grid_spec=pltpu.PrefetchScalarGridSpec(
            num_scalar_prefetch=1, grid=(),
            in_specs=[hbm] * 4 + [vm] * 4, out_specs=[vm, vm],
            scratch_shapes=[
                pltpu.VMEM((total, width), BF16),
                pltpu.VMEM((kv, total, dim), BF16),
                pltpu.VMEM((kv, dim, total), BF16),
                pltpu.VMEM((kv, groups * piece, dim), BF16),
                pltpu.VMEM((kv, 1, groups * piece), F32),
                pltpu.VMEM((kv, 1, groups * piece), F32),
                pltpu.VMEM((kv, dim, groups * piece), F32),
                pltpu.SemaphoreType.DMA((8,)),
            ]),
        out_shape=[jax.ShapeDtypeStruct((total, heads * dim), BF16), jax.ShapeDtypeStruct((heads, total), F32)],
        compiler_params=params(0),
        cost_estimate=cost(2 * flops, 4 * total * width, heads * total * total // 2),
        name="attend",
    )(table, *blocks, cos2, sin2, q_norm, k_norm)


def attend_back_kernel(s_ref, a0, a1, a2, a3, g0, g1, g2, g3, o_hbm, lse_ref, cos_ref, sin_ref, qg_ref, kg_ref,
                       out_ref, gain_ref, raw, dout, o_ref, kf, kt, qf, dof, dk, dv, dqt, sems, *,
                       dim, kv, groups, piece, n_dev):
    qw, kw = kv * groups * dim, kv * dim
    n_piece = 2 * n_dev
    scale = dim ** -0.5
    copies = gather_pieces(s_ref, (a0, a1, a2, a3), raw, sems, piece, n_dev)
    copies += gather_pieces(s_ref, (g0, g1, g2, g3), dout, sems.at[pl.ds(8, 8)], piece, n_dev)
    copies.append(pltpu.make_async_copy(o_hbm, o_ref, sems.at[16]))
    for copy in copies:
        copy.start()
    for copy in copies:
        copy.wait()
    k_gain = 1.0 + kg_ref[...]
    q_gain = 1.0 + qg_ref[...]

    def rows_of(idx):
        return pl.ds(pl.multiple_of(idx * piece, piece), piece)

    def prepare(idx, carry):
        here = rows_of(idx)
        cos2, sin2 = cos_ref[here, :], sin_ref[here, :]
        for h in range(kv):
            unit, _ = unit_of(raw[here, qw + h * dim:qw + (h + 1) * dim])
            final = rope_fwd(unit * k_gain, cos2, sin2).astype(BF16)
            kf[h, here, :] = final
            kt[h, :, here] = final.astype(F32).T.astype(BF16)
        return carry

    lax.fori_loop(0, n_piece, prepare, 0)
    gain_ref[...] = jnp.zeros_like(gain_ref)

    def norm_back(d_final, raw_vals, gain, cos2, sin2, slot):
        unit, inv = unit_of(raw_vals)
        d_scaled = rope_bwd(d_final, cos2, sin2)
        gain_ref[slot:slot + 1, :] += jnp.sum(d_scaled * unit, axis=0, keepdims=True)
        d_unit = d_scaled * gain
        return (inv * (d_unit - unit * jnp.mean(d_unit * unit, axis=-1, keepdims=True))).astype(BF16)

    def query_piece(p, carry):
        here = rows_of(p)
        there = rows_of(slot_of(p, n_dev))
        cos2, sin2 = cos_ref[here, :], sin_ref[here, :]
        lse_rows, delta_rows = [], []
        for h in range(kv):
            lses, deltas = [], []
            for g in range(groups):
                head = h * groups + g
                cols = slice(head * dim, (head + 1) * dim)
                rows = slice(g * piece, (g + 1) * piece)
                qf[h, rows, :] = final_head(raw[here, cols], q_gain, cos2, sin2)
                d_o = dout[here, cols]
                dof[h, rows, :] = d_o
                prod = d_o.astype(F32) * o_ref[there, cols].astype(F32)
                deltas.append(jnp.sum(prod.T, axis=0, keepdims=True))
                lses.append(lse_ref[head:head + 1, here])
            lse_rows.append(jnp.concatenate(lses, axis=1))
            delta_rows.append(jnp.concatenate(deltas, axis=1))

        def block(idx, h, first, mask):
            keys = rows_of(idx)
            k_blk = kf[h, keys, :]
            v_blk = raw[keys, qw + kw + h * dim:qw + kw + (h + 1) * dim]
            q_all, do_all = qf[h], dof[h]
            prob = jnp.exp2(mm(k_blk, q_all, NT) * (scale * LOG2E) - lse_rows[h])
            if mask is not None:
                prob = jnp.where(mask, prob, 0.0)
            d_sc = (prob * (mm(v_blk, do_all, NT) - delta_rows[h])).astype(BF16)
            dv_part = mm(prob.astype(BF16), do_all)
            dk_part = mm(d_sc, q_all)
            dq_part = mm(kt[h, :, keys], d_sc)
            if first:
                dv[h, keys, :] = dv_part
                dk[h, keys, :] = dk_part
                dqt[h] = dq_part
            else:
                dv[h, keys, :] += dv_part
                dk[h, keys, :] += dk_part
                dqt[h] += dq_part

        mask = causal_t(piece, groups)
        for h in range(kv):
            block(p, h, True, mask)

        def inner(j, c):
            for h in range(kv):
                block(j, h, False, None)
            return c

        lax.fori_loop(0, p, inner, 0)
        for h in range(kv):
            for g in range(groups):
                head = h * groups + g
                cols = slice(head * dim, (head + 1) * dim)
                d_q = dqt[h, :, g * piece:(g + 1) * piece].T * scale
                out_ref[there, cols] = norm_back(d_q, raw[here, cols], q_gain, cos2, sin2, 0)
        return carry

    lax.fori_loop(0, n_piece, query_piece, 0)

    def finish(idx, carry):
        here = rows_of(idx)
        there = rows_of(slot_of(idx, n_dev))
        cos2, sin2 = cos_ref[here, :], sin_ref[here, :]
        for h in range(kv):
            cols = slice(qw + h * dim, qw + (h + 1) * dim)
            out_ref[there, cols] = norm_back(dk[h, here, :] * scale, raw[here, cols], k_gain, cos2, sin2, 1)
            out_ref[there, qw + kw + h * dim:qw + kw + (h + 1) * dim] = dv[h, here, :].astype(BF16)
        return carry

    lax.fori_loop(0, n_piece, finish, 0)


def attend_back(table, blocks, d_blocks, out, lse, cos2, sin2, q_norm, k_norm, dim, kv, groups):
    seq = blocks[0].shape[0]
    n_dev = len(blocks)
    width = blocks[0].shape[1]
    total, piece, heads = seq * n_dev, seq // 2, kv * groups
    vm = pl.BlockSpec(memory_space=pltpu.VMEM)
    hbm = pl.BlockSpec(memory_space=pl.ANY)
    flops = 10 * heads * dim * total * total * 9 / 16
    return pl.pallas_call(
        functools.partial(attend_back_kernel, dim=dim, kv=kv, groups=groups, piece=piece, n_dev=n_dev),
        grid_spec=pltpu.PrefetchScalarGridSpec(
            num_scalar_prefetch=1, grid=(),
            in_specs=[hbm] * 9 + [vm] * 5, out_specs=[vm, vm],
            scratch_shapes=[
                pltpu.VMEM((total, width), BF16),
                pltpu.VMEM((total, heads * dim), BF16),
                pltpu.VMEM((total, heads * dim), BF16),
                pltpu.VMEM((kv, total, dim), BF16),
                pltpu.VMEM((kv, dim, total), BF16),
                pltpu.VMEM((kv, groups * piece, dim), BF16),
                pltpu.VMEM((kv, groups * piece, dim), BF16),
                pltpu.VMEM((kv, total, dim), F32),
                pltpu.VMEM((kv, total, dim), F32),
                pltpu.VMEM((kv, dim, groups * piece), F32),
                pltpu.SemaphoreType.DMA((17,)),
            ]),
        out_shape=[jax.ShapeDtypeStruct((total, width), BF16), jax.ShapeDtypeStruct((8, dim), F32)],
        compiler_params=params(0),
        cost_estimate=cost(2 * flops, 6 * total * width, heads * total * total // 2),
        name="attend_back",
    )(table, *blocks, *d_blocks, out, lse, cos2, sin2, q_norm, k_norm)


def out_kernel(s_ref, own_ref, far_ref, w_own_ref, w_far_ref, x_ref, dy_ref, wpost_ref, *rest):
    y_ref, datt_ref, dpost_ref, acc = rest[-4:]
    step = pl.program_id(1)
    rows = acc.shape[0]

    @pl.when(step == 0)
    def _():
        acc[...] = mm(own_ref[...], w_own_ref[...])

    @pl.when((step > 0) & (step < 4))
    def _():
        acc[...] += mm(own_ref[...], w_own_ref[...])

    @pl.when(step >= 4)
    def _():
        acc[...] += mm(far_ref[...], w_far_ref[...])

    @pl.when(step == 7)
    def _():
        gain = 1.0 + wpost_ref[...]

        @pl.when(pl.program_id(0) == 0)
        def _():
            dpost_ref[...] = jnp.zeros_like(dpost_ref)

        def chunk(k, carry):
            here = pl.ds(pl.multiple_of(k * 16, 16), 16)
            vals = acc[here, :]
            inv = lax.rsqrt(jnp.mean(vals * vals, axis=-1, keepdims=True) + EPS)
            unit = vals * inv
            y_ref[0, here, :] = (x_ref[0, here, :].astype(F32) + unit * gain).astype(BF16)
            grad = dy_ref[0, here, :].astype(F32)
            prod = grad * unit
            dpost_ref[...] += prod[:8] + prod[8:]
            d_unit = grad * gain
            datt_ref[here, :] = (inv * (d_unit - unit * jnp.mean(d_unit * unit, axis=-1, keepdims=True))).astype(BF16)
            return carry

        lax.fori_loop(0, rows // 16, chunk, 0)


def project_out(table, own, far, w_own, w_far, hidden, cotangent, w_post, batch, y_prev):
    n_batch, seq, width = hidden.shape
    depth = own.shape[1] // 4
    tile = 384
    near = lambda t, k, s: (t, jnp.minimum(k, 3))
    away = lambda t, k, s: (t, jnp.maximum(k - 4, 0))

    def w_away(t, k, s):
        rel = jnp.maximum(k - 4, 0)
        return (2 * (rel % 2) + (s[S_X] + rel // 2) % 2, 0)

    once = pl.Buffered(1)
    act = lambda t, k, s: (batch, t, 0)
    in_specs = [
        pl.BlockSpec((tile, depth), near),
        pl.BlockSpec((tile, depth), away),
        pl.BlockSpec((depth, width), lambda t, k, s: (s[S_BLOCK + jnp.minimum(k, 3)], 0)),
        pl.BlockSpec((depth, width), w_away),
        pl.BlockSpec((1, tile, width), act, pipeline_mode=once),
        pl.BlockSpec((1, tile, width), act, pipeline_mode=once),
        pl.BlockSpec((1, width), lambda t, k, s: (0, 0)),
    ]
    args = [table, own, far, w_own, w_far, hidden, cotangent, w_post]
    alias = {}
    if y_prev is not None:
        in_specs.append(pl.BlockSpec(memory_space=pl.ANY))
        args.append(y_prev)
        alias = {8: 0}
    return pl.pallas_call(
        out_kernel,
        grid_spec=pltpu.PrefetchScalarGridSpec(
            num_scalar_prefetch=1, grid=(seq // tile, 8),
            in_specs=in_specs,
            out_specs=[
                pl.BlockSpec((1, tile, width), act),
                pl.BlockSpec((tile, width), lambda t, k, s: (t, 0)),
                pl.BlockSpec((8, width), lambda t, k, s: (0, 0)),
            ],
            scratch_shapes=[pltpu.VMEM((tile, width), F32)],
        ),
        out_shape=[jax.ShapeDtypeStruct((n_batch, seq, width), BF16), jax.ShapeDtypeStruct((seq, width), BF16),
                   jax.ShapeDtypeStruct((8, width), F32)],
        input_output_aliases=alias,
        compiler_params=params(2),
        cost_estimate=cost(2 * seq * width * depth * 8, 8 * seq * width + 32 * depth * width),
        name="project_out",
    )(*args)


def dout_kernel(s_ref, d_ref, w_ref, *outs):
    peer = pl.program_id(0)
    for rel in range(4):
        @pl.when(peer == rel)
        def _(out=outs[rel]):
            out[...] = mm(d_ref[...], w_ref[...], NT).astype(BF16)


def heads_grad(table, d_attn, w_o, n_blocks):
    seq, width = d_attn.shape
    depth = w_o.shape[0] // n_blocks
    tile = 384
    return pl.pallas_call(
        dout_kernel,
        grid_spec=pltpu.PrefetchScalarGridSpec(
            num_scalar_prefetch=1, grid=(n_blocks, seq // tile),
            in_specs=[pl.BlockSpec((tile, width), lambda r, t, s: (t, 0)),
                      pl.BlockSpec((depth, width), lambda r, t, s: (s[S_BLOCK + r], 0))],
            out_specs=[pl.BlockSpec((tile, depth), functools.partial(
                lambda r, t, s, rel: (jnp.where(r < rel, 0, jnp.where(r == rel, t, seq // tile - 1)), 0), rel=rel))
                for rel in range(n_blocks)],
        ),
        out_shape=[jax.ShapeDtypeStruct((seq, depth), BF16)] * n_blocks,
        compiler_params=params(2),
        cost_estimate=cost(2 * seq * width * depth * n_blocks, 2 * (seq * width * 4 + depth * width * n_blocks)),
        name="heads_grad",
    )(table, d_attn, w_o)


def din_kernel(s_ref, d0, d1, d2, d3, wq_ref, wk_ref, wv_ref, keep_ref, send_ref, dq, dk, dv):
    qw, kw = dq.shape[1] // 4, dk.shape[1] // 4
    half = keep_ref.shape[0]

    @pl.when(pl.program_id(0) == 0)
    def _():
        for rel, src in enumerate((d0, d1, d2, d3)):
            blk = s_ref[S_BLOCK + rel]
            for part in range(2):
                start = ((s_ref[S_TP] + part) % 2) * half
                rows = pl.ds(pl.multiple_of(start, half), half)
                to = slice(part * half, (part + 1) * half)
                dq[to, pl.ds(pl.multiple_of(blk * qw, qw), qw)] = src[rows, :qw]
                dk[to, pl.ds(pl.multiple_of(blk * kw, kw), kw)] = src[rows, qw:qw + kw]
                dv[to, pl.ds(pl.multiple_of(blk * kw, kw), kw)] = src[rows, qw + kw:]

    out = mm(dq[...], wq_ref[...], NT) + mm(dk[...], wk_ref[...], NT) + mm(dv[...], wv_ref[...], NT)
    keep_ref[...] = out[:half]
    send_ref[...] = out[half:]


def input_grad(table, grads, w_q, w_k, w_v, seq):
    width = w_q.shape[0]
    block = grads[0].shape[1]
    tile = 896
    return pl.pallas_call(
        din_kernel,
        grid_spec=pltpu.PrefetchScalarGridSpec(
            num_scalar_prefetch=1, grid=(width // tile,),
            in_specs=[pl.BlockSpec((seq, block), lambda n, s: (s[S_DEV], 0))] * 4 + [
                pl.BlockSpec((tile, w.shape[1]), lambda n, s: (n, 0)) for w in (w_q, w_k, w_v)],
            out_specs=[pl.BlockSpec((seq // 2, tile), lambda n, s: (0, n))] * 2,
            scratch_shapes=[pltpu.VMEM((seq, w.shape[1]), BF16) for w in (w_q, w_k, w_v)],
        ),
        out_shape=[jax.ShapeDtypeStruct((seq // 2, width), F32)] * 2,
        compiler_params=params(1),
        cost_estimate=cost(2 * seq * width * block * 4, 2 * width * block * 4 + 4 * seq * width),
        name="input_grad",
    )(table, *grads, w_q, w_k, w_v)


def dx_kernel(s_ref, keep_ref, got_ref, x_ref, dy_ref, wpre_ref, dx_ref, dpre_ref):
    gain = 1.0 + wpre_ref[...]

    @pl.when(pl.program_id(0) == 0)
    def _():
        dpre_ref[...] = jnp.zeros_like(dpre_ref)

    def chunk(k, carry):
        here = pl.ds(pl.multiple_of(k * 16, 16), 16)
        xf = x_ref[0, here, :].astype(F32)
        inv = lax.rsqrt(jnp.mean(xf * xf, axis=-1, keepdims=True) + EPS)
        unit = xf * inv
        d_normed = keep_ref[here, :] + got_ref[here, :]
        prod = d_normed * unit
        dpre_ref[...] += prod[:8] + prod[8:]
        d_unit = d_normed * gain
        back = inv * (d_unit - unit * jnp.mean(d_unit * unit, axis=-1, keepdims=True))
        dx_ref[here, :] = (dy_ref[0, here, :].astype(F32) + back).astype(BF16)
        return carry

    lax.fori_loop(0, keep_ref.shape[0] // 16, chunk, 0)


def finish_dx(table, keep, got, hidden, cotangent, w_pre, batch):
    half, width = keep.shape
    tile = 96
    steps = half // tile
    row = lambda t, s: (t, 0)
    act = lambda t, s: (batch, s[S_TP] * steps + t, 0)
    return pl.pallas_call(
        dx_kernel,
        grid_spec=pltpu.PrefetchScalarGridSpec(
            num_scalar_prefetch=1, grid=(steps,),
            in_specs=[pl.BlockSpec((tile, width), row), pl.BlockSpec((tile, width), row),
                      pl.BlockSpec((1, tile, width), act), pl.BlockSpec((1, tile, width), act),
                      pl.BlockSpec((1, width), lambda t, s: (0, 0))],
            out_specs=[pl.BlockSpec((tile, width), row), pl.BlockSpec((8, width), lambda t, s: (0, 0))],
        ),
        out_shape=[jax.ShapeDtypeStruct((half, width), BF16), jax.ShapeDtypeStruct((8, width), F32)],
        compiler_params=params(1),
        cost_estimate=cost(20 * half * width, 14 * half * width),
        name="finish_dx",
    )(table, keep, got, hidden, cotangent, w_pre)


def stream(pieces, col, buf, sems, step, slot):
    for idx, src in enumerate(pieces):
        @pl.when(step == idx)
        def _(src=src):
            pltpu.make_async_copy(src.at[:, col], buf.at[slot], sems.at[slot]).start()


def dw_in_kernel(s_ref, *refs):
    n_piece = 8
    pieces, grads = refs[:n_piece], refs[n_piece:n_piece + 2]
    wq_ref, wk_ref, wv_ref, buf, sems = refs[-5:]
    m_idx, step = pl.program_id(0), pl.program_id(1)
    tile = buf.shape[2]
    slot = (m_idx * n_piece + step) % 2
    qw, kw = wq_ref.shape[1], wk_ref.shape[1]

    def columns(m):
        return pl.ds(pl.multiple_of((s_ref[S_CORE] * pl.num_programs(0) + m) * tile, tile), tile)

    @pl.when((m_idx == 0) & (step == 0))
    def _():
        stream(pieces, columns(0), buf, sems, step, slot)

    @pl.when(step < n_piece - 1)
    def _():
        stream(pieces, columns(m_idx), buf, sems, step + 1, 1 - slot)

    @pl.when((step == n_piece - 1) & (m_idx < pl.num_programs(0) - 1))
    def _():
        stream(pieces, columns(m_idx + 1), buf, sems, 0, 1 - slot)

    pltpu.make_async_copy(pieces[0].at[:, columns(0)], buf.at[slot], sems.at[slot]).wait()
    lhs = buf[slot]

    def accumulate(rhs):
        for ref, cols in ((wq_ref, slice(0, qw)), (wk_ref, slice(qw, qw + kw)), (wv_ref, slice(qw + kw, qw + 2 * kw))):
            part = mm(lhs, rhs[:, cols], TN)

            @pl.when(step == 0)
            def _(ref=ref, part=part):
                ref[...] = part

            @pl.when(step > 0)
            def _(ref=ref, part=part):
                ref[...] += part

    @pl.when(step % 2 == 0)
    def _():
        accumulate(grads[0])

    @pl.when(step % 2 == 1)
    def _():
        accumulate(grads[1])


def weight_grad_in(table, normed, grads, shapes, rel, prev):
    seq, width = normed[0].shape
    block = grads[0].shape[1]
    half = width // 2
    tile = 896
    hbm = pl.BlockSpec(memory_space=pl.ANY)
    widths = [w // 4 for w in shapes]
    in_specs = [hbm] * 8 + [
        pl.BlockSpec((seq, block), lambda m, k, s: (s[S_PEER + k // 2], 0)),
        pl.BlockSpec((seq, block), lambda m, k, s: (s[S_PEER + k // 2], 0))]
    args = [table, *normed, *grads]
    alias = {}
    if prev is not None:
        in_specs += [hbm] * 3
        alias = {len(args) + idx: idx for idx in range(3)}
        args += list(prev)
    return pl.pallas_call(
        dw_in_kernel,
        grid_spec=pltpu.PrefetchScalarGridSpec(
            num_scalar_prefetch=1, grid=(half // tile, 8),
            in_specs=in_specs,
            out_specs=[pl.BlockSpec((tile, w), lambda m, k, s: (m, s[S_BLOCK + rel])) for w in widths],
            scratch_shapes=[pltpu.VMEM((2, seq, tile), BF16), pltpu.SemaphoreType.DMA((2,))],
        ),
        out_shape=[jax.ShapeDtypeStruct((half, w), F32) for w in shapes],
        input_output_aliases=alias,
        compiler_params=params(2),
        cost_estimate=cost(2 * 8 * seq * half * block, 16 * seq * half + 3 * 16 * seq * block + 4 * half * block),
        name="weight_grad_in",
    )(*args)


def dw_out_kernel(s_ref, *refs):
    n_piece = 8
    pieces, outs = refs[:n_piece], refs[n_piece:n_piece + 2]
    dw_ref, buf, sems = refs[-3:]
    n_idx, step = pl.program_id(0), pl.program_id(1)
    tile = buf.shape[2]
    slot = (n_idx * n_piece + step) % 2

    def columns(n):
        return pl.ds(pl.multiple_of(n * tile, tile), tile)

    @pl.when((n_idx == 0) & (step == 0))
    def _():
        stream(pieces, columns(0), buf, sems, step, slot)

    @pl.when(step < n_piece - 1)
    def _():
        stream(pieces, columns(n_idx), buf, sems, step + 1, 1 - slot)

    @pl.when((step == n_piece - 1) & (n_idx < pl.num_programs(0) - 1))
    def _():
        stream(pieces, columns(n_idx + 1), buf, sems, 0, 1 - slot)

    pltpu.make_async_copy(pieces[0].at[:, columns(0)], buf.at[slot], sems.at[slot]).wait()
    rhs = buf[slot]

    for which in range(2):
        @pl.when((step % 2 == which) & (step == 0))
        def _(lhs=outs[which]):
            dw_ref[...] = mm(lhs[...], rhs, TN)

        @pl.when((step % 2 == which) & (step > 0))
        def _(lhs=outs[which]):
            dw_ref[...] += mm(lhs[...], rhs, TN)


def weight_grad_out(table, d_attn, outs, rel, prev):
    seq, width = d_attn[0].shape
    depth = outs[0].shape[1]
    tile = width // 3
    hbm = pl.BlockSpec(memory_space=pl.ANY)
    in_specs = [hbm] * 8 + [
        pl.BlockSpec((seq, depth), lambda n, k, s: (s[S_PEER + k // 2], 0)),
        pl.BlockSpec((seq, depth), lambda n, k, s: (s[S_PEER + k // 2], 0))]
    args = [table, *d_attn, *outs]
    alias = {}
    if prev is not None:
        in_specs.append(hbm)
        alias = {len(args): 0}
        args.append(prev)
    return pl.pallas_call(
        dw_out_kernel,
        grid_spec=pltpu.PrefetchScalarGridSpec(
            num_scalar_prefetch=1, grid=(width // tile, 8),
            in_specs=in_specs,
            out_specs=pl.BlockSpec((depth, tile), lambda n, k, s: ((s[S_X] + rel // 2) % 2, n)),
            scratch_shapes=[pltpu.VMEM((2, seq, tile), BF16), pltpu.SemaphoreType.DMA((2,))],
        ),
        out_shape=jax.ShapeDtypeStruct((2 * depth, width), F32),
        input_output_aliases=alias,
        compiler_params=params(2),
        cost_estimate=cost(2 * 8 * seq * width * depth, 16 * seq * width + 48 * seq * depth + 4 * depth * width),
        name="weight_grad_out",
    )(*args)


def solution(mesh):
    n_cp = mesh.shape['cp']
    hops = {rel: [(dev, dev ^ rel) for dev in range(n_cp)] for rel in range(1, n_cp)}
    cores = [[0, 1], [2, 3]]

    def per_device(hidden, cotangent, pos_loc, w_q, w_k, w_v, w_o, w_pre, w_post, q_norm, k_norm):
        dim = q_norm.shape[0]
        n_batch, seq, width = hidden.shape
        kv = w_k.shape[1] // dim // n_cp
        groups = w_q.shape[1] // w_k.shape[1]
        depth = kv * groups * dim
        dev, tp = lax.axis_index('cp'), lax.axis_index('tp')
        core, x_idx = dev % 2, dev // 2
        peers = [dev ^ rel for rel in range(n_cp)]
        blocks = [2 * (p % 2) + p // 2 for p in peers]
        table = jnp.stack([jnp.asarray(v, jnp.int32) for v in [dev, tp, core, x_idx] + peers + blocks])

        def move(val, rel):
            return lax.ppermute(val, 'cp', hops[rel])

        def swap(val):
            return lax.ppermute(val, 'tp', [(0, 1), (1, 0)])

        pre2, post2 = w_pre[None, :], w_post[None, :]
        qn2, kn2 = q_norm[None, :], k_norm[None, :]

        far_half = swap(lax.dynamic_slice(w_o, (core * 2 * depth, 0), (2 * depth, width)))
        w_far = jnp.concatenate([far_half, move(far_half, 1)], axis=0)

        pos_all = lax.all_gather(pos_loc, 'cp', tiled=True).reshape(n_cp, 2, seq // 2)
        pos_log = jnp.concatenate([pos_all[:, 0].reshape(-1), pos_all[::-1, 1].reshape(-1)])
        inv_freq = 1.0 / (ROPE_SCALE * ROPE_BASE ** (jnp.arange(dim // 2, dtype=F32) * (2.0 / dim)))
        angles = pos_log.astype(F32)[:, None] * inv_freq[None, :]
        cos_t, sin_t = jnp.cos(angles), jnp.sin(angles)
        cos2 = jnp.concatenate([cos_t, cos_t], axis=1)
        sin2 = jnp.concatenate([-sin_t, sin_t], axis=1)

        normed, raws, outs, lses, lhs_own, lhs_far = [], [], [], [], [], []
        for b in range(n_batch):
            got = project(table, hidden, pre2, w_q, w_k, w_v, b, n_cp)
            normed.append(got[0])
            raws.append([got[1]] + [move(got[1 + rel], rel) for rel in range(1, n_cp)])

        out_x = []
        for b in range(n_batch):
            o_b, lse_b = attend(table, raws[b], cos2, sin2, qn2, kn2, dim, kv, groups)
            outs.append(o_b)
            lses.append(lse_b)
            o_x = move(o_b, 2)
            out_x.append(o_x)

            def rows(val, who):
                return lax.dynamic_slice(val, (who * seq, 0), (seq, val.shape[1]))

            side = move(jnp.concatenate([rows(o_b, peers[1]), rows(o_x, peers[1])], axis=1), 1)
            own = jnp.concatenate([rows(o_b, dev), side[:, :depth], rows(o_x, dev), side[:, depth:]], axis=1)
            lhs_own.append(own)
            lhs_far.append(swap(own))

        y_out, d_attn, d_post = None, [], 0.0
        for b in range(n_batch):
            y_out, da, dp = project_out(table, lhs_own[b], lhs_far[b], w_o, w_far, hidden, cotangent, post2, b, y_out)
            d_attn.append(da)
            d_post = d_post + jnp.sum(dp, axis=0)

        grads, gains = [], 0.0
        for b in range(n_batch):
            d_heads = heads_grad(table, d_attn[b], w_o, n_cp)
            d_blocks = [d_heads[0]] + [move(d_heads[rel], rel) for rel in range(1, n_cp)]
            g_b, gain_b = attend_back(table, raws[b], d_blocks, outs[b], lses[b], cos2, sin2, qn2, kn2, dim, kv, groups)
            g_x = move(g_b, 2)
            grads.append([g_b, move(g_b, 1), g_x, move(g_x, 1)])
            gains = gains + gain_b

        def everyone(vals):
            far = [move(v, 2) for v in vals]
            near = [move(v, 1) for v in vals]
            diag = [move(v, 1) for v in far]
            return [v for quad in zip(*[[a, b2, c2, d2] for a, b2, c2, d2 in zip(vals, near, far, diag)]) for v in quad]

        normed_all = everyone(normed)
        d_attn_all = everyone(d_attn)

        dx_full = jnp.zeros((n_batch, seq, width), BF16)
        d_pre = 0.0
        for b in range(n_batch):
            keep, send = input_grad(table, grads[b], w_q, w_k, w_v, seq)
            dx_b, dp = finish_dx(table, keep, swap(send), hidden, cotangent, pre2, b)
            d_pre = d_pre + jnp.sum(dp, axis=0)
            dx_full = lax.dynamic_update_slice(dx_full, dx_b[None], (b, tp * (seq // 2), 0))
            dx_full = lax.dynamic_update_slice(dx_full, swap(dx_b)[None], (b, (1 - tp) * (seq // 2), 0))

        d_wo = None
        for rel, os in ((0, outs), (2, out_x)):
            d_wo = weight_grad_out(table, d_attn_all, os, rel, d_wo)
        d_in = None
        for rel in (0, 2, 1, 3):
            d_in = weight_grad_in(table, normed_all, [g[rel] for g in grads],
                                  (w_q.shape[1], w_k.shape[1], w_v.shape[1]), rel, d_in)

        def join(val):
            return lax.all_gather(val, 'cp', axis_index_groups=cores, tiled=True)

        d_wo, d_wq, d_wk, d_wv = join(d_wo), join(d_in[0]), join(d_in[1]), join(d_in[2])
        d_post = jnp.where(tp == 0, d_post, 0.0)
        d_post, d_pre, d_qn, d_kn = lax.psum((d_post, d_pre, gains[0], gains[1]), ('tp', 'cp'))
        return y_out, dx_full, d_wq, d_wk, d_wv, d_wo, d_pre, d_post, d_qn, d_kn

    specs_in = (P('dp', 'cp', None), P('dp', 'cp', None), P(('dp', 'cp')), P(None, 'tp'), P(None, 'tp'), P(None, 'tp'),
                P('tp', None), P(None), P(None), P(None), P(None))
    specs_out = (P('dp', 'cp', None), P('dp', 'cp', None), P('dp', 'tp'), P('dp', 'tp'), P('dp', 'tp'),
                 P(('dp', 'tp'), None), P('dp'), P('dp'), P('dp'), P('dp'))
    return jax.shard_map(per_device, mesh=mesh, in_specs=specs_in, out_specs=specs_out, check_vma=False)
```

time: 5710 us -> 2700 us (0.47)
  waiting for transfers between devices: 3640 us -> 1020 us
  matrix products: 1270 us -> 0 us
  Pallas kernels: 0 us -> 1210 us
  other arithmetic: 358 us -> 12.1 us
  blocking collectives: 36.4 us -> 249 us
  local copies, waits for them, and re-layouts: 369 us -> 163 us
    psum x4 -> x0, waiting for transfers between devices: 3300 us -> none  [the longest x1 1430 us: per_device(): lax.psum(jnp.einsum('bsd,bsh->dh', normed, dq_bf, preferred_element_type=...]
    dot_general x39 -> x0, matrix products: 1270 us -> none  [the longest x4 176 us: grad_block(): jnp.einsum('bkgqd,bskd->bkgqs', d_out, v_blk, preferred_element_type=jnp....]
    pallas_call x0 -> x20, Pallas kernels: none -> 1210 us  [the longest x4 326 us: weight_grad_in(): pl.pallas_call(dw_in_kernel, grid_spec=pltpu.PrefetchScalarGridSpec(num_s...]
    ppermute x26 -> x42, waiting for transfers between devices: 337 us -> 1020 us  [the longest x35 645 us: move(): return lax.ppermute(val, 'cp', hops[rel])]
    reduce_sum x15 -> x4, other arithmetic: 203 us -> 1.11 us  [the longest x2 1.02 us: per_device(): d_pre = d_pre + jnp.sum(dp, axis=0)]
    psum x2 -> x1, blocking collectives: 36.4 us -> 177 us  [per_device(): lax.psum((d_post, d_pre, gains[0], gains[1]), ('tp', 'cp'))]
    while x63 -> x0, local copies, waits for them, and re-layouts: 93 us -> none
    all_gather x0 -> x1, blocking collectives: none -> 71.9 us  [per_device(): lax.all_gather(pos_loc, 'cp', tiled=True).reshape(n_cp, 2, seq // 2)]
  transfers between devices with their start and end apart: 30 -> 46, of which waited for: 17 -> 13; matrix products, arithmetic and copies ran while one was open for 16% -> 2% of each run, Pallas kernels for 0% -> 42%
where the time goes in v1:
time: 2700 us; the launch traced here: 2690 us
  Pallas kernels  1210 us (45%)
  waiting for transfers between devices  1020 us (38%)
  blocking collectives  249 us (9%)
  local copies, waits for them, and re-layouts  163 us (6%)
    ppermute x35, waiting for transfers between devices, move(): return lax.ppermute(val, 'cp', hops[rel])  645 us
    ppermute x7, waiting for transfers between devices, swap(): return lax.ppermute(val, 'tp', [(0, 1), (1, 0)])  374 us
    pallas_call x4, Pallas kernels, weight_grad_in(): pl.pallas_call(dw_in_kernel, grid_spec=pltpu.PrefetchScalarGridSpec(num_s...  326 us
    psum x1, blocking collectives, per_device(): lax.psum((d_post, d_pre, gains[0], gains[1]), ('tp', 'cp'))  177 us
    pallas_call x2, Pallas kernels, attend_back(): pl.pallas_call(functools.partial(attend_back_kernel, dim=dim, kv=kv, grou...  176 us
    pallas_call x2, Pallas kernels, project_out(): pl.pallas_call(out_kernel, grid_spec=pltpu.PrefetchScalarGridSpec(num_sca...  150 us
    pallas_call x2, Pallas kernels, attend(): pl.pallas_call(functools.partial(attend_kernel, dim=dim, kv=kv, groups=gr...  136 us
    unnamed x58, local copies, waits for them, and re-layouts  118 us
  transfers between devices with their start and end apart: 46, of which 13 were waited for; matrix products, arithmetic and copies ran while one was open for 2% of the time, Pallas kernels for 42%

profile of v1, /device:TPU:0, one launch (start us, length us, event | category | flops | bytes accessed | tf_op | source)
XLA Modules:
  0.0 2691.2 jit_solution(10499331537311246091)
XLA Ops:
  7.3 9.5 constant_dynamic-slice_fusion.4
  16.8 3.4 collective-permute-start.6
  21.5 57.8 %qkv.2 = (bf16[768,5376]{1,0:T(8,128)(2,1)}, bf16[768,1024]{1,0:T(8,128)(2,1)}, bf16[768,1024]{1,0:T(8,128)(2,1)}, bf16[768,1024]{1,0:T(8,128)(2,1)}, bf16[768,1024]{1,0:T(8,128)(2,1)}) custom-call(s32[12]{0:T(128)} %stack.48.s_ref, bf16[2,768,5376]{2,1,0:T(8,128)(2,1)} %x_ref.11, f32[1,5376]{1,0:T(1,128)} %broadcast_in_dim.33.wpre_ref, ...), custom_call_target="tpu_custom_call" | custom-call | flops 33822867456 | bytes 104595456 | tf_op jit(solution)/shard_map/qkv/pallas_call | solution.py:73
  79.3 58.5 %qkv.3 = (bf16[768,5376]{1,0:T(8,128)(2,1)}, bf16[768,1024]{1,0:T(8,128)(2,1)}, bf16[768,1024]{1,0:T(8,128)(2,1)}, bf16[768,1024]{1,0:T(8,128)(2,1)}, bf16[768,1024]{1,0:T(8,128)(2,1)}) custom-call(s32[12]{0:T(128)} %stack.48.s_ref, bf16[2,768,5376]{2,1,0:T(8,128)(2,1)} %x_ref.11, f32[1,5376]{1,0:T(1,128)} %broadcast_in_dim.33.wpre_ref, ...), custom_call_target="tpu_custom_call" | custom-call | flops 33822867456 | bytes 104595456 | tf_op jit(solution)/shard_map/qkv/pallas_call | solution.py:73
  139.7 71.9 %all-gather = s32[4,1,768]{2,1,0:T(1,128)S(1)} all-gather(s32[1,1,768]{2,1,0:T(1,128)S(1)} %reshape.48), channel_id=1, replica_groups=mesh['dp'=1,'tp'=2,'cp'=4] {'cp'}, dimensions={0}, use_global_device_ids=true | all-gather | bytes 15360 | tf_op jit(solution)/shard_map/all_gather | solution.py:782
  211.8 5.8 fusion
  217.7 39.1 %collective-permute-done.6 = bf16[1024,5376]{1,0:T(8,128)(2,1)} collective-permute-done((bf16[1024,5376]{1,0:T(8,128)(2,1)}, bf16[1024,5376]{1,0:T(8,128)(2,1)}, u32[]{:S(2)}, u32[]{:S(2)}) %collective-permute-start.6) | collective-permute-done | bytes 11010080 | tf_op jit(solution)/shard_map/ppermute | solution.py:774
  261.2 67.9 %attend.3 = (bf16[3072,512]{1,0:T(8,128)(2,1)}, f32[4,3072]{1,0:T(4,128)}) custom-call(s32[12]{0:T(128)} %stack.48.s_ref, bf16[768,1024]{1,0:T(8,128)(2,1)} %get-tuple-element.67.a0, bf16[768,1024]{1,0:T(8,128)(2,1)} %copy-done.20, bf16[768,1024]{1,0:T(8,128)(2,1)} %collective-permute-done.9.a2, bf16[768,1024]{1,0:T(8,128)(2,1)} %collective-permute-done.10.a3, ...), custom_call_target="tpu_custom_call" | custom-call | flops 21743271936 | bytes 12582912 | tf_op jit(solution)/shard_map/attend/pallas_call | solution.py:227
  332.0 68.3 %attend.2 = (bf16[3072,512]{1,0:T(8,128)(2,1)}, f32[4,3072]{1,0:T(4,128)}) custom-call(s32[12]{0:T(128)} %stack.48.s_ref, bf16[768,1024]{1,0:T(8,128)(2,1)} %get-tuple-element.62.a0, bf16[768,1024]{1,0:T(8,128)(2,1)} %copy-done.19, bf16[768,1024]{1,0:T(8,128)(2,1)} %collective-permute-done.1.a2, bf16[768,1024]{1,0:T(8,128)(2,1)} %collective-permute-done.2.a3, ...), custom_call_target="tpu_custom_call" | custom-call | flops 21743271936 | bytes 12582912 | tf_op jit(solution)/shard_map/attend/pallas_call | solution.py:227
  403.2 67.2 %collective-permute-done.3.refs_9_ = bf16[3072,512]{1,0:T(8,128)(2,1)} collective-permute-done((bf16[3072,512]{1,0:T(8,128)(2,1)}, bf16[3072,512]{1,0:T(8,128)(2,1)}, u32[]{:S(2)}, u32[]{:S(2)}) %collective-permute-start.3) | collective-permute-done | bytes 3145760 | tf_op jit(solution)/shard_map/ppermute | solution.py:771
  479.4 9.9 constant_dynamic-update-slice_fusion.1
  489.3 9.5 constant_dynamic-update-slice_fusion.w_far_ref
  498.9 44.8 %collective-permute-done.13.far_ref = bf16[768,2048]{1,0:T(8,128)(2,1)} collective-permute-done((bf16[768,2048]{1,0:T(8,128)(2,1)S(1)}, bf16[768,2048]{1,0:T(8,128)(2,1)}, u32[]{:S(2)}, u32[]{:S(2)}) %collective-permute-start.13) | collective-permute-done | bytes 3145760 | tf_op jit(solution)/shard_map/ppermute | solution.py:774
  543.7 75.1 %project_out.2 = (bf16[2,768,5376]{2,1,0:T(8,128)(2,1)}, bf16[768,5376]{1,0:T(8,128)(2,1)}, f32[8,5376]{1,0:T(8,128)}) custom-call(s32[12]{0:T(128)} %stack.48.s_ref, bf16[768,2048]{1,0:T(8,128)(2,1)} %copy-done.3, bf16[768,2048]{1,0:T(8,128)(2,1)} %collective-permute-done.13.far_ref, bf16[2048,5376]{1,0:T(8,128)(2,1)} %w_ref.3, ...), custom_call_target="tpu_custom_call" | custom-call | flops 33822867456 | bytes 121110528 | tf_op jit(solution)/shard_map/project_out/pallas_call | solution.py:464
  618.8 29.3 %heads_grad.2 = (bf16[768,512]{1,0:T(8,128)(2,1)}, bf16[768,512]{1,0:T(8,128)(2,1)}, bf16[768,512]{1,0:T(8,128)(2,1)}, bf16[768,512]{1,0:T(8,128)(2,1)}) custom-call(s32[12]{0:T(128)} %stack.48.s_ref, bf16[768,5376]{1,0:T(8,128)(2,1)} %get-tuple-element.74.d_ref.refs_0_, bf16[2048,5376]{1,0:T(8,128)(2,1)} %w_ref.3), custom_call_target="tpu_custom_call" | custom-call | flops 16911433728 | bytes 55050240 | tf_op jit(solution)/shard_map/heads_grad/pallas_call | solution.py:497
  650.0 75.4 %project_out.3 = (bf16[2,768,5376]{2,1,0:T(8,128)(2,1)}, bf16[768,5376]{1,0:T(8,128)(2,1)}, f32[8,5376]{1,0:T(8,128)}) custom-call(s32[12]{0:T(128)} %stack.48.s_ref, bf16[768,2048]{1,0:T(8,128)(2,1)} %pad_maximum_fusion.own_ref, bf16[768,2048]{1,0:T(8,128)(2,1)} %collective-permute-done.5.far_ref, ...), custom_call_target="tpu_custom_call", output_to_operand_aliasing={{0}: (8, {})} | custom-call | flops 33822867456 | bytes 121110528 | tf_op jit(solution)/shard_map/project_out/pallas_call | solution.py:464
  725.4 29.4 %heads_grad.3 = (bf16[768,512]{1,0:T(8,128)(2,1)}, bf16[768,512]{1,0:T(8,128)(2,1)}, bf16[768,512]{1,0:T(8,128)(2,1)}, bf16[768,512]{1,0:T(8,128)(2,1)}) custom-call(s32[12]{0:T(128)} %stack.48.s_ref, bf16[768,5376]{1,0:T(8,128)(2,1)} %get-tuple-element.84.d_ref.refs_1_, bf16[2048,5376]{1,0:T(8,128)(2,1)} %w_ref.3), custom_call_target="tpu_custom_call" | custom-call | flops 16911433728 | bytes 55050240 | tf_op jit(solution)/shard_map/heads_grad/pallas_call | solution.py:497
  755.3 76.4 %collective-permute-done.33.refs_5_ = bf16[768,5376]{1,0:T(8,128)(2,1)} collective-permute-done((bf16[768,5376]{1,0:T(8,128)(2,1)}, bf16[768,5376]{1,0:T(8,128)(2,1)}, u32[]{:S(2)}, u32[]{:S(2)}) %collective-permute-start.33) | collective-permute-done | bytes 8257568 | tf_op jit(solution)/shard_map/ppermute | solution.py:771
  832.3 16.3 collective-permute-done.15.g2
  848.6 15.3 collective-permute-done.16.g3
  865.3 16.2 collective-permute-done.23.g2
  881.5 88.1 %attend_back.2 = (bf16[3072,1024]{1,0:T(8,128)(2,1)}, f32[8,128]{1,0:T(8,128)}) custom-call(s32[12]{0:T(128)} %stack.48.s_ref, bf16[768,1024]{1,0:T(8,128)(2,1)} %get-tuple-element.67.a0, bf16[768,1024]{1,0:T(8,128)(2,1)} %copy-done.20, bf16[768,1024]{1,0:T(8,128)(2,1)} %collective-permute-done.9.a2, bf16[768,1024]{1,0:T(8,128)(2,1)} %collective-permute-done.10.a3, ...), custom_call_target="tpu_custom_call" | custom-call | flops 54358179840 | bytes 18874368 | tf_op jit(solution)/shard_map/attend_back/pallas_call | solution.py:370
  970.6 87.8 %attend_back.3 = (bf16[3072,1024]{1,0:T(8,128)(2,1)}, f32[8,128]{1,0:T(8,128)}) custom-call(s32[12]{0:T(128)} %stack.48.s_ref, bf16[768,1024]{1,0:T(8,128)(2,1)} %get-tuple-element.62.a0, bf16[768,1024]{1,0:T(8,128)(2,1)} %copy-done.19, bf16[768,1024]{1,0:T(8,128)(2,1)} %collective-permute-done.1.a2, bf16[768,1024]{1,0:T(8,128)(2,1)} %collective-permute-done.2.a3, ...), custom_call_target="tpu_custom_call" | custom-call | flops 54358179840 | bytes 18874368 | tf_op jit(solution)/shard_map/attend_back/pallas_call | solution.py:370
  1060.0 81.7 %weight_grad_in.4 = (f32[2688,2048]{1,0:T(8,128)}, f32[2688,1024]{1,0:T(8,128)}, f32[2688,1024]{1,0:T(8,128)}) custom-call(s32[12]{0:T(128)} %stack.48.s_ref, bf16[768,5376]{1,0:T(8,128)(2,1)} %get-tuple-element.94.refs_0_, bf16[768,5376]{1,0:T(8,128)(2,1)} %get-tuple-element.95.refs_1_, bf16[768,5376]{1,0:T(8,128)(2,1)} %collective-permute-done.30.refs_2_, ...), custom_call_target="tpu_custom_call" | custom-call | flops 33822867456 | bytes 81788928 | tf_op jit(solution)/shard_map/weight_grad_in/pallas_call | solution.py:671
  1141.8 100.7 %collective-permute-done.26.d2.refs_9_ = bf16[3072,1024]{1,0:T(8,128)(2,1)} collective-permute-done((bf16[3072,1024]{1,0:T(8,128)(2,1)}, bf16[3072,1024]{1,0:T(8,128)(2,1)}, u32[]{:S(2)}, u32[]{:S(2)}) %collective-permute-start.26) | collective-permute-done | bytes 6291488 | tf_op jit(solution)/shard_map/ppermute | solution.py:771
  1242.5 81.3 %weight_grad_in.5 = (f32[2688,2048]{1,0:T(8,128)}, f32[2688,1024]{1,0:T(8,128)}, f32[2688,1024]{1,0:T(8,128)}) custom-call(s32[12]{0:T(128)} %stack.48.s_ref, bf16[768,5376]{1,0:T(8,128)(2,1)} %get-tuple-element.94.refs_0_, bf16[768,5376]{1,0:T(8,128)(2,1)} %get-tuple-element.95.refs_1_, ...), custom_call_target="tpu_custom_call", output_to_operand_aliasing={{0}: (11, {}), {1}: (12, {}), {2}: (13, {})} | custom-call | flops 33822867456 | bytes 81788928 | tf_op jit(solution)/shard_map/weight_grad_in/pallas_call | solution.py:671
  1323.8 81.4 %weight_grad_in.6 = (f32[2688,2048]{1,0:T(8,128)}, f32[2688,1024]{1,0:T(8,128)}, f32[2688,1024]{1,0:T(8,128)}) custom-call(s32[12]{0:T(128)} %stack.48.s_ref, bf16[768,5376]{1,0:T(8,128)(2,1)} %get-tuple-element.94.refs_0_, bf16[768,5376]{1,0:T(8,128)(2,1)} %get-tuple-element.95.refs_1_, ...), custom_call_target="tpu_custom_call", output_to_operand_aliasing={{0}: (11, {}), {1}: (12, {}), {2}: (13, {})} | custom-call | flops 33822867456 | bytes 81788928 | tf_op jit(solution)/shard_map/weight_grad_in/pallas_call | solution.py:671
  1405.3 81.3 %weight_grad_in.7 = (f32[2688,2048]{1,0:T(8,128)}, f32[2688,1024]{1,0:T(8,128)}, f32[2688,1024]{1,0:T(8,128)}) custom-call(s32[12]{0:T(128)} %stack.48.s_ref, bf16[768,5376]{1,0:T(8,128)(2,1)} %get-tuple-element.94.refs_0_, bf16[768,5376]{1,0:T(8,128)(2,1)} %get-tuple-element.95.refs_1_, ...), custom_call_target="tpu_custom_call", output_to_operand_aliasing={{0}: (11, {}), {1}: (12, {}), {2}: (13, {})} | custom-call | flops 33822867456 | bytes 81788928 | tf_op jit(solution)/shard_map/weight_grad_in/pallas_call | solution.py:671
  1490.7 178.0 %collective-permute-done.38.refs_4_ = bf16[768,5376]{1,0:T(8,128)(2,1)S(1)} collective-permute-done((bf16[768,5376]{1,0:T(8,128)(2,1)}, bf16[768,5376]{1,0:T(8,128)(2,1)S(1)}, u32[]{:S(2)}, u32[]{:S(2)}) %collective-permute-start.38) | collective-permute-done | bytes 8257568 | tf_op jit(solution)/shard_map/ppermute | solution.py:771
  1672.0 173.2 %collective-permute-done.39.refs_5_ = bf16[768,5376]{1,0:T(8,128)(2,1)S(1)} collective-permute-done((bf16[768,5376]{1,0:T(8,128)(2,1)}, bf16[768,5376]{1,0:T(8,128)(2,1)S(1)}, u32[]{:S(2)}, u32[]{:S(2)}) %collective-permute-start.39) | collective-permute-done | bytes 8257568 | tf_op jit(solution)/shard_map/ppermute | solution.py:771
  1845.2 3.3 copy-done.15
  1858.1 56.5 %weight_grad_out.2.refs_10_ = f32[1024,5376]{1,0:T(8,128)} custom-call(s32[12]{0:T(128)} %stack.48.s_ref, bf16[768,5376]{1,0:T(8,128)(2,1)} %get-tuple-element.74.d_ref.refs_0_, bf16[768,5376]{1,0:T(8,128)(2,1)} %get-tuple-element.84.d_ref.refs_1_, bf16[768,5376]{1,0:T(8,128)(2,1)} %copy-done.16, bf16[768,5376]{1,0:T(8,128)(2,1)} %copy-done.17, ...), custom_call_target="tpu_custom_call" | custom-call | flops 33822867456 | bytes 95944704 | tf_op jit(solution)/shard_map/weight_grad_out/pallas_call | solution.py:737
  1914.6 56.3 %weight_grad_out.3 = f32[1024,5376]{1,0:T(8,128)} custom-call(s32[12]{0:T(128)} %stack.48.s_ref, bf16[768,5376]{1,0:T(8,128)(2,1)} %get-tuple-element.74.d_ref.refs_0_, bf16[768,5376]{1,0:T(8,128)(2,1)} %get-tuple-element.84.d_ref.refs_1_, bf16[768,5376]{1,0:T(8,128)(2,1)} %copy-done.16, ...), custom_call_target="tpu_custom_call", output_to_operand_aliasing={{}: (11, {})} | custom-call | flops 33822867456 | bytes 95944704 | tf_op jit(solution)/shard_map/weight_grad_out/pallas_call | solution.py:737
  1971.0 49.0 %input_grad.2 = (f32[384,5376]{1,0:T(8,128)}, f32[384,5376]{1,0:T(8,128)}) custom-call(s32[12]{0:T(128)} %stack.48.s_ref, bf16[3072,1024]{1,0:T(8,128)(2,1)} %get-tuple-element.80.d0.refs_8_, bf16[3072,1024]{1,0:T(8,128)(2,1)} %collective-permute-done.17.d1.refs_8_, bf16[3072,1024]{1,0:T(8,128)(2,1)} %collective-permute-done.18.d2.refs_8_, ...), custom_call_target="tpu_custom_call" | custom-call | flops 33822867456 | bytes 60555264 | tf_op jit(solution)/shard_map/input_grad/pallas_call | solution.py:539
  2020.3 48.8 %input_grad.3 = (f32[384,5376]{1,0:T(8,128)}, f32[384,5376]{1,0:T(8,128)}) custom-call(s32[12]{0:T(128)} %stack.48.s_ref, bf16[3072,1024]{1,0:T(8,128)(2,1)} %get-tuple-element.90.d0.refs_9_, bf16[3072,1024]{1,0:T(8,128)(2,1)} %collective-permute-done.25.d1.refs_9_, bf16[3072,1024]{1,0:T(8,128)(2,1)} %collective-permute-done.26.d2.refs_9_, ...), custom_call_target="tpu_custom_call" | custom-call | flops 33822867456 | bytes 60555264 | tf_op jit(solution)/shard_map/input_grad/pallas_call | solution.py:539
  2070.9 129.6 %collective-permute-done.20.got_ref = f32[384,5376]{1,0:T(8,128)} collective-permute-done((f32[384,5376]{1,0:T(8,128)}, f32[384,5376]{1,0:T(8,128)}, u32[]{:S(2)}, u32[]{:S(2)}) %collective-permute-start.20) | collective-permute-done | bytes 8257568 | tf_op jit(solution)/shard_map/ppermute | solution.py:774
  2200.5 15.9 finish_dx.2
  2216.9 160.6 %collective-permute-done.28.got_ref = f32[384,5376]{1,0:T(8,128)} collective-permute-done((f32[384,5376]{1,0:T(8,128)}, f32[384,5376]{1,0:T(8,128)}, u32[]{:S(2)}, u32[]{:S(2)}) %collective-permute-start.28) | collective-permute-done | bytes 8257568 | tf_op jit(solution)/shard_map/ppermute | solution.py:774
  2377.5 16.1 finish_dx.3
  2394.9 177.0 %all-reduce = (f32[5376]{0:T(1024)}, f32[5376]{0:T(1024)}, f32[128]{0:T(128)}, f32[128]{0:T(128)}) all-reduce(f32[5376]{0:T(1024)S(1)} %add.83, f32[5376]{0:T(1024)S(1)} %add_select_fusion, f32[128]{0:T(128)S(1)} %get-tuple-element.136, f32[128]{0:T(128)S(1)} %get-tuple-element.135), channel_id=1, replica_groups=mesh['dp'=1,'tp'=2,'cp'=4] {'tp','cp'}, use_global_device_ids=true, to_apply=%region_2.3 | all-reduce | flops 11008 | bytes 88064 | tf_op jit(solution)/shard_map/psum | solution.py:858
  2572.0 6.6 broadcast_in_dim.37
  2581.0 4.8 bitcast_dynamic-update-slice_fusion.2
  2588.0 4.4 bitcast_dynamic-update-slice_fusion
  2592.5 32.0 %copy.52 = f32[5376,2048]{1,0:T(8,128)} copy(f32[5376,2048]{1,0:T(8,128)} %all-gather.6.cloned.1.call-done) | data formatting | bytes 88080384
  2624.5 17.6 copy.53
  2642.0 3.7 copy-done
  2645.7 7.9 copy.54
  2653.6 30.5 %copy.55 = f32[2048,5376]{1,0:T(8,128)} copy(f32[2048,5376]{1,0:T(8,128)} %all-gather.12.cloned.1.call-done) | data formatting | bytes 88080384
  (166 shorter events, 54.8 us)
Async XLA Ops:
  7.2 2585.3 %all-gather.8.cloned.1.call-start = ((), (), s32[]{:S(2)}) async-start(), calls=%async_computation.1 | async-start | bytes 33030144 | tf_op jit(solution)/shard_map/all_gather | solution.py:854
  16.8 240.0 %collective-permute-start.6 = (bf16[1024,5376]{1,0:T(8,128)(2,1)}, bf16[1024,5376]{1,0:T(8,128)(2,1)}, u32[]{:S(2)}, u32[]{:S(2)}) collective-permute-start(bf16[1024,5376]{1,0:T(8,128)(2,1)} %constant_dynamic-slice_fusion.4), channel_id=1, source_target_pairs={{0,4},{4,0},{1,5},{5,1},{2,6},{6,2},{3,7},{7,3}} | collective-permute-start | bytes 33030152 | tf_op jit(solution)/shard_map/ppermute | solution.py:774
  79.3 251.5 %collective-permute-start = (bf16[768,1024]{1,0:T(8,128)(2,1)}, bf16[768,1024]{1,0:T(8,128)(2,1)S(1)}, u32[]{:S(2)}, u32[]{:S(2)}) collective-permute-start(bf16[768,1024]{1,0:T(8,128)(2,1)} %get-tuple-element.63), channel_id=1, source_target_pairs={{0,1},{1,0},{2,3},{3,2},{4,5},{5,4},{6,7},{7,6}} | collective-permute-start | bytes 4718600 | tf_op jit(solution)/shard_map/ppermute | solution.py:771
  137.8 121.5 %collective-permute-start.8 = (bf16[768,1024]{1,0:T(8,128)(2,1)}, bf16[768,1024]{1,0:T(8,128)(2,1)S(1)}, u32[]{:S(2)}, u32[]{:S(2)}) collective-permute-start(bf16[768,1024]{1,0:T(8,128)(2,1)} %get-tuple-element.68), channel_id=1, source_target_pairs={{0,1},{1,0},{2,3},{3,2},{4,5},{5,4},{6,7},{7,6}} | collective-permute-start | bytes 4718600 | tf_op jit(solution)/shard_map/ppermute | solution.py:771
  138.3 122.7 %collective-permute-start.9 = (bf16[768,1024]{1,0:T(8,128)(2,1)}, bf16[768,1024]{1,0:T(8,128)(2,1)}, u32[]{:S(2)}, u32[]{:S(2)}) collective-permute-start(bf16[768,1024]{1,0:T(8,128)(2,1)} %get-tuple-element.69), channel_id=1, source_target_pairs={{0,2},{1,3},{2,0},{3,1},{4,6},{5,7},{6,4},{7,5}} | collective-permute-start | bytes 4718600 | tf_op jit(solution)/shard_map/ppermute | solution.py:771
  139.7 121.4 %collective-permute-start.10 = (bf16[768,1024]{1,0:T(8,128)(2,1)}, bf16[768,1024]{1,0:T(8,128)(2,1)}, u32[]{:S(2)}, u32[]{:S(2)}) collective-permute-start(bf16[768,1024]{1,0:T(8,128)(2,1)} %get-tuple-element.70), channel_id=1, source_target_pairs={{0,3},{1,2},{2,1},{3,0},{4,7},{5,6},{6,5},{7,4}} | collective-permute-start | bytes 4718600 | tf_op jit(solution)/shard_map/ppermute | solution.py:771
  256.8 232.5 %collective-permute-start.7 = (bf16[1024,5376]{1,0:T(8,128)(2,1)}, bf16[1024,5376]{1,0:T(8,128)(2,1)}, u32[]{:S(2)}, u32[]{:S(2)}) collective-permute-start(bf16[1024,5376]{1,0:T(8,128)(2,1)} %collective-permute-done.6), channel_id=1, source_target_pairs={{0,1},{1,0},{2,3},{3,2},{4,5},{5,4},{6,7},{7,6}} | collective-permute-start | bytes 33030152 | tf_op jit(solution)/shard_map/ppermute | solution.py:771
  259.3 71.5 %collective-permute-start.1 = (bf16[768,1024]{1,0:T(8,128)(2,1)}, bf16[768,1024]{1,0:T(8,128)(2,1)}, u32[]{:S(2)}, u32[]{:S(2)}) collective-permute-start(bf16[768,1024]{1,0:T(8,128)(2,1)} %get-tuple-element.64), channel_id=1, source_target_pairs={{0,2},{1,3},{2,0},{3,1},{4,6},{5,7},{6,4},{7,5}} | collective-permute-start | bytes 4718600 | tf_op jit(solution)/shard_map/ppermute | solution.py:771
  261.0 69.8 %collective-permute-start.2 = (bf16[768,1024]{1,0:T(8,128)(2,1)}, bf16[768,1024]{1,0:T(8,128)(2,1)}, u32[]{:S(2)}, u32[]{:S(2)}) collective-permute-start(bf16[768,1024]{1,0:T(8,128)(2,1)} %get-tuple-element.65), channel_id=1, source_target_pairs={{0,3},{1,2},{2,1},{3,0},{4,7},{5,6},{6,5},{7,4}} | collective-permute-start | bytes 4718600 | tf_op jit(solution)/shard_map/ppermute | solution.py:771
  329.1 71.7 %collective-permute-start.11 = (bf16[3072,512]{1,0:T(8,128)(2,1)}, bf16[3072,512]{1,0:T(8,128)(2,1)}, u32[]{:S(2)}, u32[]{:S(2)}) collective-permute-start(bf16[3072,512]{1,0:T(8,128)(2,1)} %get-tuple-element.71.o_hbm.refs_8_), channel_id=1, source_target_pairs={{0,2},{1,3},{2,0},{3,1},{4,6},{5,7},{6,4},{7,5}} | collective-permute-start | bytes 9437192 | tf_op jit(solution)/shard_map/ppermute | solution.py:771
  400.4 70.0 %collective-permute-start.3 = (bf16[3072,512]{1,0:T(8,128)(2,1)}, bf16[3072,512]{1,0:T(8,128)(2,1)}, u32[]{:S(2)}, u32[]{:S(2)}) collective-permute-start(bf16[3072,512]{1,0:T(8,128)(2,1)} %get-tuple-element.66.o_hbm.refs_9_), channel_id=1, source_target_pairs={{0,2},{1,3},{2,0},{3,1},{4,6},{5,7},{6,4},{7,5}} | collective-permute-start | bytes 9437192 | tf_op jit(solution)/shard_map/ppermute | solution.py:771
  402.7 69.4 %collective-permute-start.12 = (bf16[768,1024]{1,0:T(8,128)(2,1)S(1)}, bf16[768,1024]{1,0:T(8,128)(2,1)S(1)}, u32[]{:S(2)}, u32[]{:S(2)}) collective-permute-start(bf16[768,1024]{1,0:T(8,128)(2,1)S(1)} %pad_maximum_fusion.5), channel_id=1, source_target_pairs={{0,1},{1,0},{2,3},{3,2},{4,5},{5,4},{6,7},{7,6}} | collective-permute-start | bytes 4718600 | tf_op jit(solution)/shard_map/ppermute | solution.py:771
  472.1 4.8 collective-permute-start.4
  472.7 71.0 %collective-permute-start.13 = (bf16[768,2048]{1,0:T(8,128)(2,1)S(1)}, bf16[768,2048]{1,0:T(8,128)(2,1)}, u32[]{:S(2)}, u32[]{:S(2)}) collective-permute-start(bf16[768,2048]{1,0:T(8,128)(2,1)S(1)} %pad_maximum_fusion.1.own_ref), channel_id=1, source_target_pairs={{0,4},{4,0},{1,5},{5,1},{2,6},{6,2},{3,7},{7,3}} | collective-permute-start | bytes 9437192 | tf_op jit(solution)/shard_map/ppermute | solution.py:774
  474.2 280.6 %collective-permute-start.32 = (bf16[768,5376]{1,0:T(8,128)(2,1)}, bf16[768,5376]{1,0:T(8,128)(2,1)}, u32[]{:S(2)}, u32[]{:S(2)}) collective-permute-start(bf16[768,5376]{1,0:T(8,128)(2,1)} %get-tuple-element.94.refs_0_), channel_id=1, source_target_pairs={{0,2},{1,3},{2,0},{3,1},{4,6},{5,7},{6,4},{7,5}} | collective-permute-start | bytes 24772616 | tf_op jit(solution)/shard_map/ppermute | solution.py:771
  474.8 356.9 %collective-permute-start.33 = (bf16[768,5376]{1,0:T(8,128)(2,1)}, bf16[768,5376]{1,0:T(8,128)(2,1)}, u32[]{:S(2)}, u32[]{:S(2)}) collective-permute-start(bf16[768,5376]{1,0:T(8,128)(2,1)} %get-tuple-element.95.refs_1_), channel_id=1, source_target_pairs={{0,2},{1,3},{2,0},{3,1},{4,6},{5,7},{6,4},{7,5}} | collective-permute-start | bytes 24772616 | tf_op jit(solution)/shard_map/ppermute | solution.py:771
  478.9 169.6 %collective-permute-start.5 = (bf16[768,2048]{1,0:T(8,128)(2,1)}, bf16[768,2048]{1,0:T(8,128)(2,1)}, u32[]{:S(2)}, u32[]{:S(2)}) collective-permute-start(bf16[768,2048]{1,0:T(8,128)(2,1)} %pad_maximum_fusion.own_ref), channel_id=1, source_target_pairs={{0,4},{4,0},{1,5},{5,1},{2,6},{6,2},{3,7},{7,3}} | collective-permute-start | bytes 9437192 | tf_op jit(solution)/shard_map/ppermute | solution.py:774
  648.2 184.1 %collective-permute-start.14 = (bf16[768,512]{1,0:T(8,128)(2,1)}, bf16[768,512]{1,0:T(8,128)(2,1)S(1)}, u32[]{:S(2)}, u32[]{:S(2)}) collective-permute-start(bf16[768,512]{1,0:T(8,128)(2,1)} %get-tuple-element.76), channel_id=1, source_target_pairs={{0,1},{1,0},{2,3},{3,2},{4,5},{5,4},{6,7},{7,6}} | collective-permute-start | bytes 2359304 | tf_op jit(solution)/shard_map/ppermute | solution.py:771
  648.2 200.4 %collective-permute-start.15 = (bf16[768,512]{1,0:T(8,128)(2,1)}, bf16[768,512]{1,0:T(8,128)(2,1)S(1)}, u32[]{:S(2)}, u32[]{:S(2)}) collective-permute-start(bf16[768,512]{1,0:T(8,128)(2,1)} %get-tuple-element.77), channel_id=1, source_target_pairs={{0,2},{1,3},{2,0},{3,1},{4,6},{5,7},{6,4},{7,5}} | collective-permute-start | bytes 2359304 | tf_op jit(solution)/shard_map/ppermute | solution.py:771
  648.5 215.4 %collective-permute-start.16 = (bf16[768,512]{1,0:T(8,128)(2,1)}, bf16[768,512]{1,0:T(8,128)(2,1)S(1)}, u32[]{:S(2)}, u32[]{:S(2)}) collective-permute-start(bf16[768,512]{1,0:T(8,128)(2,1)} %get-tuple-element.78), channel_id=1, source_target_pairs={{0,3},{1,2},{2,1},{3,0},{4,7},{5,6},{6,5},{7,4}} | collective-permute-start | bytes 2359304 | tf_op jit(solution)/shard_map/ppermute | solution.py:771
  754.8 110.4 %collective-permute-start.22 = (bf16[768,512]{1,0:T(8,128)(2,1)}, bf16[768,512]{1,0:T(8,128)(2,1)S(1)}, u32[]{:S(2)}, u32[]{:S(2)}) collective-permute-start(bf16[768,512]{1,0:T(8,128)(2,1)} %get-tuple-element.86), channel_id=1, source_target_pairs={{0,1},{1,0},{2,3},{3,2},{4,5},{5,4},{6,7},{7,6}} | collective-permute-start | bytes 2359304 | tf_op jit(solution)/shard_map/ppermute | solution.py:771
  831.7 49.8 %collective-permute-start.23 = (bf16[768,512]{1,0:T(8,128)(2,1)}, bf16[768,512]{1,0:T(8,128)(2,1)S(1)}, u32[]{:S(2)}, u32[]{:S(2)}) collective-permute-start(bf16[768,512]{1,0:T(8,128)(2,1)} %get-tuple-element.87), channel_id=1, source_target_pairs={{0,2},{1,3},{2,0},{3,1},{4,6},{5,7},{6,4},{7,5}} | collective-permute-start | bytes 2359304 | tf_op jit(solution)/shard_map/ppermute | solution.py:771
  832.3 226.1 %collective-permute-start.30 = (bf16[768,5376]{1,0:T(8,128)(2,1)}, bf16[768,5376]{1,0:T(8,128)(2,1)}, u32[]{:S(2)}, u32[]{:S(2)}) collective-permute-start(bf16[768,5376]{1,0:T(8,128)(2,1)} %get-tuple-element.94.refs_0_), channel_id=1, source_target_pairs={{0,1},{1,0},{2,3},{3,2},{4,5},{5,4},{6,7},{7,6}} | collective-permute-start | bytes 24772616 | tf_op jit(solution)/shard_map/ppermute | solution.py:771
  848.6 211.0 %collective-permute-start.31 = (bf16[768,5376]{1,0:T(8,128)(2,1)}, bf16[768,5376]{1,0:T(8,128)(2,1)}, u32[]{:S(2)}, u32[]{:S(2)}) collective-permute-start(bf16[768,5376]{1,0:T(8,128)(2,1)} %get-tuple-element.95.refs_1_), channel_id=1, source_target_pairs={{0,1},{1,0},{2,3},{3,2},{4,5},{5,4},{6,7},{7,6}} | collective-permute-start | bytes 24772616 | tf_op jit(solution)/shard_map/ppermute | solution.py:771
  863.9 195.7 %collective-permute-start.34 = (bf16[768,5376]{1,0:T(8,128)(2,1)}, bf16[768,5376]{1,0:T(8,128)(2,1)}, u32[]{:S(2)}, u32[]{:S(2)}) collective-permute-start(bf16[768,5376]{1,0:T(8,128)(2,1)} %collective-permute-done.32.refs_4_), channel_id=1, source_target_pairs={{0,1},{1,0},{2,3},{3,2},{4,5},{5,4},{6,7},{7,6}} | collective-permute-start | bytes 24772616 | tf_op jit(solution)/shard_map/ppermute | solution.py:771
  865.2 104.4 %copy-start.23 = (bf16[768,512]{1,0:T(8,128)(2,1)}, bf16[768,512]{1,0:T(8,128)(2,1)S(1)}, u32[]{:S(2)}) copy-start(bf16[768,512]{1,0:T(8,128)(2,1)S(1)} %collective-permute-done.22.g1) | copy-start | bytes 2359300
  865.2 194.8 %collective-permute-start.35 = (bf16[768,5376]{1,0:T(8,128)(2,1)}, bf16[768,5376]{1,0:T(8,128)(2,1)}, u32[]{:S(2)}, u32[]{:S(2)}) collective-permute-start(bf16[768,5376]{1,0:T(8,128)(2,1)} %collective-permute-done.33.refs_5_), channel_id=1, source_target_pairs={{0,1},{1,0},{2,3},{3,2},{4,5},{5,4},{6,7},{7,6}} | collective-permute-start | bytes 24772616 | tf_op jit(solution)/shard_map/ppermute | solution.py:771
  881.5 88.1 %copy-start.25 = (bf16[768,512]{1,0:T(8,128)(2,1)}, bf16[768,512]{1,0:T(8,128)(2,1)S(1)}, u32[]{:S(2)}) copy-start(bf16[768,512]{1,0:T(8,128)(2,1)S(1)} %collective-permute-done.23.g2) | copy-start | bytes 2359300
  881.5 88.1 %collective-permute-start.24 = (bf16[768,512]{1,0:T(8,128)(2,1)}, bf16[768,512]{1,0:T(8,128)(2,1)}, u32[]{:S(2)}, u32[]{:S(2)}) collective-permute-start(bf16[768,512]{1,0:T(8,128)(2,1)} %get-tuple-element.88), channel_id=1, source_target_pairs={{0,3},{1,2},{2,1},{3,0},{4,7},{5,6},{6,5},{7,4}} | collective-permute-start | bytes 2359304 | tf_op jit(solution)/shard_map/ppermute | solution.py:771
  969.6 172.1 %collective-permute-start.18 = (bf16[3072,1024]{1,0:T(8,128)(2,1)}, bf16[3072,1024]{1,0:T(8,128)(2,1)}, u32[]{:S(2)}, u32[]{:S(2)}) collective-permute-start(bf16[3072,1024]{1,0:T(8,128)(2,1)} %get-tuple-element.80.d0.refs_8_), channel_id=1, source_target_pairs={{0,2},{1,3},{2,0},{3,1},{4,6},{5,7},{6,4},{7,5}} | collective-permute-start | bytes 18874376 | tf_op jit(solution)/shard_map/ppermute | solution.py:771
  1058.4 184.1 %collective-permute-start.26 = (bf16[3072,1024]{1,0:T(8,128)(2,1)}, bf16[3072,1024]{1,0:T(8,128)(2,1)}, u32[]{:S(2)}, u32[]{:S(2)}) collective-permute-start(bf16[3072,1024]{1,0:T(8,128)(2,1)} %get-tuple-element.90.d0.refs_9_), channel_id=1, source_target_pairs={{0,2},{1,3},{2,0},{3,1},{4,6},{5,7},{6,4},{7,5}} | collective-permute-start | bytes 18874376 | tf_op jit(solution)/shard_map/ppermute | solution.py:771
  1059.5 264.3 %collective-permute-start.17 = (bf16[3072,1024]{1,0:T(8,128)(2,1)}, bf16[3072,1024]{1,0:T(8,128)(2,1)}, u32[]{:S(2)}, u32[]{:S(2)}) collective-permute-start(bf16[3072,1024]{1,0:T(8,128)(2,1)} %get-tuple-element.80.d0.refs_8_), channel_id=1, source_target_pairs={{0,1},{1,0},{2,3},{3,2},{4,5},{5,4},{6,7},{7,6}} | collective-permute-start | bytes 18874376 | tf_op jit(solution)/shard_map/ppermute | solution.py:771
  1059.6 264.2 %collective-permute-start.25 = (bf16[3072,1024]{1,0:T(8,128)(2,1)}, bf16[3072,1024]{1,0:T(8,128)(2,1)}, u32[]{:S(2)}, u32[]{:S(2)}) collective-permute-start(bf16[3072,1024]{1,0:T(8,128)(2,1)} %get-tuple-element.90.d0.refs_9_), channel_id=1, source_target_pairs={{0,1},{1,0},{2,3},{3,2},{4,5},{5,4},{6,7},{7,6}} | collective-permute-start | bytes 18874376 | tf_op jit(solution)/shard_map/ppermute | solution.py:771
  1141.7 263.6 %collective-permute-start.19 = (bf16[3072,1024]{1,0:T(8,128)(2,1)}, bf16[3072,1024]{1,0:T(8,128)(2,1)}, u32[]{:S(2)}, u32[]{:S(2)}) collective-permute-start(bf16[3072,1024]{1,0:T(8,128)(2,1)} %collective-permute-done.18.d2.refs_8_), channel_id=1, source_target_pairs={{0,1},{1,0},{2,3},{3,2},{4,5},{5,4},{6,7},{7,6}} | collective-permute-start | bytes 18874376 | tf_op jit(solution)/shard_map/ppermute | solution.py:771
  1242.5 162.8 %collective-permute-start.27 = (bf16[3072,1024]{1,0:T(8,128)(2,1)}, bf16[3072,1024]{1,0:T(8,128)(2,1)}, u32[]{:S(2)}, u32[]{:S(2)}) collective-permute-start(bf16[3072,1024]{1,0:T(8,128)(2,1)} %collective-permute-done.26.d2.refs_9_), channel_id=1, source_target_pairs={{0,1},{1,0},{2,3},{3,2},{4,5},{5,4},{6,7},{7,6}} | collective-permute-start | bytes 18874376 | tf_op jit(solution)/shard_map/ppermute | solution.py:771
  1486.6 1105.8 %all-gather.10.cloned.1.call-start = ((), (), s32[]{:S(2)}) async-start(), calls=%async_computation.2 | async-start | bytes 33030144 | tf_op jit(solution)/shard_map/all_gather | solution.py:854
  1487.4 1105.1 %all-gather.6.cloned.1.call-start = ((), (), s32[]{:S(2)}) async-start(), calls=%async_computation | async-start | bytes 66060288 | tf_op jit(solution)/shard_map/all_gather | solution.py:854
  1488.1 1104.3 %all-gather.12.cloned.1.call-start = ((), (), s32[]{:S(2)}) async-start(), calls=%async_computation.3 | async-start | bytes 66060288 | tf_op jit(solution)/shard_map/all_gather | solution.py:854
  1488.1 180.5 %collective-permute-start.38 = (bf16[768,5376]{1,0:T(8,128)(2,1)}, bf16[768,5376]{1,0:T(8,128)(2,1)S(1)}, u32[]{:S(2)}, u32[]{:S(2)}) collective-permute-start(bf16[768,5376]{1,0:T(8,128)(2,1)} %get-tuple-element.74.d_ref.refs_0_), channel_id=1, source_target_pairs={{0,2},{1,3},{2,0},{3,1},{4,6},{5,7},{6,4},{7,5}} | collective-permute-start | bytes 24772616 | tf_op jit(solution)/shard_map/ppermute | solution.py:771
  1489.5 355.7 %collective-permute-start.39 = (bf16[768,5376]{1,0:T(8,128)(2,1)}, bf16[768,5376]{1,0:T(8,128)(2,1)S(1)}, u32[]{:S(2)}, u32[]{:S(2)}) collective-permute-start(bf16[768,5376]{1,0:T(8,128)(2,1)} %get-tuple-element.84.d_ref.refs_1_), channel_id=1, source_target_pairs={{0,2},{1,3},{2,0},{3,1},{4,6},{5,7},{6,4},{7,5}} | collective-permute-start | bytes 24772616 | tf_op jit(solution)/shard_map/ppermute | solution.py:771
  1490.2 355.0 %collective-permute-start.36 = (bf16[768,5376]{1,0:T(8,128)(2,1)}, bf16[768,5376]{1,0:T(8,128)(2,1)S(1)}, u32[]{:S(2)}, u32[]{:S(2)}) collective-permute-start(bf16[768,5376]{1,0:T(8,128)(2,1)} %get-tuple-element.74.d_ref.refs_0_), channel_id=1, source_target_pairs={{0,1},{1,0},{2,3},{3,2},{4,5},{5,4},{6,7},{7,6}} | collective-permute-start | bytes 24772616 | tf_op jit(solution)/shard_map/ppermute | solution.py:771
  1490.2 355.0 %collective-permute-start.37 = (bf16[768,5376]{1,0:T(8,128)(2,1)}, bf16[768,5376]{1,0:T(8,128)(2,1)S(1)}, u32[]{:S(2)}, u32[]{:S(2)}) collective-permute-start(bf16[768,5376]{1,0:T(8,128)(2,1)} %get-tuple-element.84.d_ref.refs_1_), channel_id=1, source_target_pairs={{0,1},{1,0},{2,3},{3,2},{4,5},{5,4},{6,7},{7,6}} | collective-permute-start | bytes 24772616 | tf_op jit(solution)/shard_map/ppermute | solution.py:771
  1672.0 173.3 %collective-permute-start.40 = (bf16[768,5376]{1,0:T(8,128)(2,1)S(1)}, bf16[768,5376]{1,0:T(8,128)(2,1)S(1)}, u32[]{:S(2)}, u32[]{:S(2)}) collective-permute-start(bf16[768,5376]{1,0:T(8,128)(2,1)S(1)} %collective-permute-done.38.refs_4_), channel_id=1, source_target_pairs={{0,1},{1,0},{2,3},{3,2},{4,5},{5,4},{6,7},{7,6}} | collective-permute-start | bytes 24772616 | tf_op jit(solution)/shard_map/ppermute | solution.py:771
  1845.2 12.9 collective-permute-start.41
  2020.0 180.5 %collective-permute-start.20 = (f32[384,5376]{1,0:T(8,128)}, f32[384,5376]{1,0:T(8,128)}, u32[]{:S(2)}, u32[]{:S(2)}) collective-permute-start(f32[384,5376]{1,0:T(8,128)} %get-tuple-element.82), channel_id=1, source_target_pairs={{0,4},{4,0},{1,5},{5,1},{2,6},{6,2},{3,7},{7,3}} | collective-permute-start | bytes 24772616 | tf_op jit(solution)/shard_map/ppermute | solution.py:774
  2069.2 308.3 %collective-permute-start.28 = (f32[384,5376]{1,0:T(8,128)}, f32[384,5376]{1,0:T(8,128)}, u32[]{:S(2)}, u32[]{:S(2)}) collective-permute-start(f32[384,5376]{1,0:T(8,128)} %get-tuple-element.92), channel_id=1, source_target_pairs={{0,4},{4,0},{1,5},{5,1},{2,6},{6,2},{3,7},{7,3}} | collective-permute-start | bytes 24772616 | tf_op jit(solution)/shard_map/ppermute | solution.py:774
  2216.4 364.5 %collective-permute-start.21 = (bf16[384,5376]{1,0:T(8,128)(2,1)}, bf16[384,5376]{1,0:T(8,128)(2,1)}, u32[]{:S(2)}, u32[]{:S(2)}) collective-permute-start(bf16[384,5376]{1,0:T(8,128)(2,1)} %get-tuple-element.83), channel_id=1, source_target_pairs={{0,4},{4,0},{1,5},{5,1},{2,6},{6,2},{3,7},{7,3}} | collective-permute-start | bytes 12386312 | tf_op jit(solution)/shard_map/ppermute | solution.py:774
  2393.6 194.4 %collective-permute-start.29 = (bf16[384,5376]{1,0:T(8,128)(2,1)}, bf16[384,5376]{1,0:T(8,128)(2,1)}, u32[]{:S(2)}, u32[]{:S(2)}) collective-permute-start(bf16[384,5376]{1,0:T(8,128)(2,1)} %get-tuple-element.93), channel_id=1, source_target_pairs={{0,4},{4,0},{1,5},{5,1},{2,6},{6,2},{3,7},{7,3}} | collective-permute-start | bytes 12386312 | tf_op jit(solution)/shard_map/ppermute | solution.py:774
  (24 other events, 408.6 us)
Sparse Core Ops, SparseCore 0:
  1486.7 44.0 all-gather.7
  1533.0 34.2 all-gather.9
  1569.4 64.0 all-gather.5
  1971.1 62.5 all-gather.11
